TPU v7x, 32 devices: a 4x2x2 block of a 4x4x8 slice. The times are simulated.
32 devices in a mesh: dp: 4 (over y, z), stage: 8 (over x, core).
Axes of the slice: x: 4, y: 2, z: 2, core: 2. Of those that a mesh axis runs over, the one named last changes fastest.
The devices are a block of a 4x4x8 slice.
Arguments:
- token_ids: int32 [32, 256], P('dp'), parts along dimension 0
- label_ids: int32 [32, 256], P('dp'), parts along dimension 0
- embedding: bfloat16 [50304, 768], P('stage')
- w_in: bfloat16 [8, 768, 3072], P('stage')
- w_out: bfloat16 [8, 3072, 768], P('stage')
Outputs:
- output 1: float32 [4], P('dp'), parts along dimension 0
- output 2: float32 [32, 768, 3072], P(('dp', 'stage')), parts along dimension 0
- output 3: float32 [32, 3072, 768], P(('dp', 'stage')), parts along dimension 0
- output 4: float32 [201216, 768], P(('dp', 'stage')), parts along dimension 0
There are 4 independent parts. A program takes and returns all parts, laid end to end along the dimension named above; an argument that names none is the same for every part.
All inputs are finite; a program needn't handle non-finite values.
Results may differ from a plain program's by a relative error of at most 0.0165463.
Values are sent between devices in bfloat16 or wider.
A program may use at most 768 MiB of HBM per device.

v0:
```python
import jax
import jax.numpy as jnp
from jax import lax
from jax.sharding import PartitionSpec as P

NORM_EPS = 1e-6


def norm_f32(act_rows):
    acts_f = act_rows.astype(jnp.float32)
    return acts_f * lax.rsqrt(jnp.mean(acts_f * acts_f, axis=-1, keepdims=True) + NORM_EPS)


def layer_forward(act_rows, w_first, w_second):
    pre_act = jnp.dot(act_rows, w_first, preferred_element_type=jnp.float32)
    hidden = jax.nn.gelu(pre_act).astype(jnp.bfloat16)
    out_f = act_rows.astype(jnp.float32) + jnp.dot(hidden, w_second, preferred_element_type=jnp.float32)
    return out_f.astype(jnp.bfloat16)


def layer_backward(act_rows, grad_out, w_first, w_second):
    pre_act = jnp.dot(act_rows, w_first, preferred_element_type=jnp.float32)
    hidden_f, gelu_pull = jax.vjp(jax.nn.gelu, pre_act)
    hidden = hidden_f.astype(jnp.bfloat16)
    grad_second = jnp.einsum("tf,td->fd", hidden, grad_out, preferred_element_type=jnp.float32)
    grad_hidden = jnp.einsum("td,fd->tf", grad_out, w_second, preferred_element_type=jnp.float32)
    grad_pre = gelu_pull(grad_hidden)[0].astype(jnp.bfloat16)
    grad_first = jnp.einsum("td,tf->df", act_rows, grad_pre, preferred_element_type=jnp.float32)
    grad_in = (grad_out.astype(jnp.float32) + jnp.einsum("tf,df->td", grad_pre, w_first, preferred_element_type=jnp.float32)).astype(jnp.bfloat16)
    return grad_in, grad_first, grad_second


def take_slot(store_arr, mb_slot):
    return lax.dynamic_index_in_dim(store_arr, mb_slot, 0, keepdims=False)


def put_slot(store_arr, new_value, mb_slot, active):
    old_value = lax.dynamic_index_in_dim(store_arr, mb_slot, 0, keepdims=False)
    return lax.dynamic_update_index_in_dim(store_arr, jnp.where(active, new_value, old_value), mb_slot, 0)


def solution(mesh):
    n_stage = mesh.shape["stage"]
    fwd_pairs = [(src_idx, src_idx + 1) for src_idx in range(n_stage - 1)]
    bwd_pairs = [(src_idx + 1, src_idx) for src_idx in range(n_stage - 1)]

    def stage_body(token_ids, label_ids, emb_rows, w_in, w_out):
        stage_idx = lax.axis_index("stage")
        is_first = stage_idx == 0
        is_last = stage_idx == n_stage - 1
        micro_count, micro_tokens = token_ids.shape
        slice_rows, model_dim = emb_rows.shape
        logit_scale = model_dim ** -0.5
        w_first = w_in[0]
        w_second = w_out[0]
        n_ticks = micro_count + n_stage - 1
        row_start = stage_idx * slice_rows
        local_tok = token_ids - row_start
        tok_here = (local_tok >= 0) & (local_tok < slice_rows)
        looked_up = jnp.take(emb_rows, jnp.clip(local_tok, 0, slice_rows - 1), axis=0)
        embedded = lax.psum(jnp.where(tok_here[..., None], looked_up, 0), "stage")
        act_zeros = jnp.zeros((micro_tokens, model_dim), jnp.bfloat16)
        store_zeros = jnp.zeros((micro_count, micro_tokens, model_dim), jnp.bfloat16)

        def fwd_tick(tick_idx, loop_carry):
            incoming, saved_in, last_out = loop_carry
            micro_idx = tick_idx - stage_idx
            active = (micro_idx >= 0) & (micro_idx < micro_count)
            mb_slot = jnp.clip(micro_idx, 0, micro_count - 1)
            act_in = jnp.where(is_first, take_slot(embedded, mb_slot), incoming)
            act_out = lax.cond(active, lambda act_val: layer_forward(act_val, w_first, w_second), lambda act_val: act_val, act_in)
            saved_in = put_slot(saved_in, act_in, mb_slot, active)
            last_out = put_slot(last_out, act_out, mb_slot, active)
            return lax.ppermute(act_out, "stage", fwd_pairs), saved_in, last_out

        _, saved_in, last_out = lax.fori_loop(0, n_ticks, fwd_tick, (act_zeros, store_zeros, store_zeros))

        normed_f, norm_pull = jax.vjp(norm_f32, last_out)
        normed = lax.psum(jnp.where(is_last, normed_f.astype(jnp.bfloat16), 0), "stage")
        local_lab = label_ids - row_start
        vocab_iota = jnp.arange(slice_rows, dtype=jnp.int32)

        def head_step(loop_carry, inputs):
            grad_rows, loss_sum = loop_carry
            normed_mb, lab_mb = inputs
            logits = jnp.einsum("td,vd->tv", normed_mb, emb_rows, preferred_element_type=jnp.float32) * logit_scale
            row_max = lax.pmax(jnp.max(logits, axis=1), "stage")
            exp_logits = jnp.exp(logits - row_max[:, None])
            is_label = lab_mb[:, None] == vocab_iota[None, :]
            row_stats = lax.psum(jnp.stack([jnp.sum(exp_logits, axis=1), jnp.sum(jnp.where(is_label, logits, 0.0), axis=1)]), "stage")
            loss_sum = loss_sum + jnp.sum(jnp.log(row_stats[0]) + row_max - row_stats[1])
            grad_logits = ((exp_logits / row_stats[0][:, None] - is_label.astype(jnp.float32)) * logit_scale).astype(jnp.bfloat16)
            grad_n = lax.psum(jnp.einsum("tv,vd->td", grad_logits, emb_rows, preferred_element_type=jnp.float32), "stage")
            grad_rows = grad_rows + jnp.einsum("tv,td->vd", grad_logits, normed_mb, preferred_element_type=jnp.float32)
            return (grad_rows, loss_sum), grad_n

        head_init = (jnp.zeros((slice_rows, model_dim), jnp.float32), jnp.zeros((), jnp.float32))
        (grad_head, loss_sum), grad_norm = lax.scan(head_step, head_init, (normed, local_lab))
        grad_last = norm_pull(grad_norm)[0]

        def run_layer(operands):
            act_rows, grad_val, acc_a, acc_b = operands
            grad_in, grad_a, grad_b = layer_backward(act_rows, grad_val, w_first, w_second)
            return grad_in, acc_a + grad_a, acc_b + grad_b

        def skip_layer(operands):
            return operands[1], operands[2], operands[3]

        def bwd_tick(tick_idx, loop_carry):
            incoming, acc_first, acc_second, grad_embedded = loop_carry
            micro_idx = tick_idx - (n_stage - 1 - stage_idx)
            active = (micro_idx >= 0) & (micro_idx < micro_count)
            mb_slot = jnp.clip(micro_idx, 0, micro_count - 1)
            grad_out = jnp.where(is_last, take_slot(grad_last, mb_slot), incoming)
            grad_in, acc_first, acc_second = lax.cond(active, run_layer, skip_layer, (take_slot(saved_in, mb_slot), grad_out, acc_first, acc_second))
            grad_embedded = put_slot(grad_embedded, grad_in, mb_slot, active)
            return lax.ppermute(grad_in, "stage", bwd_pairs), acc_first, acc_second, grad_embedded

        bwd_init = (act_zeros, jnp.zeros(w_first.shape, jnp.float32), jnp.zeros(w_second.shape, jnp.float32), store_zeros)
        _, acc_first, acc_second, grad_embedded = lax.fori_loop(0, n_ticks, bwd_tick, bwd_init)

        grad_lookup_in = lax.psum(jnp.where(is_first, grad_embedded, 0), "stage")
        seg_ids = jnp.where(tok_here, local_tok, slice_rows).reshape(-1)
        grad_lookup = jax.ops.segment_sum(grad_lookup_in.reshape(-1, model_dim).astype(jnp.float32), seg_ids, num_segments=slice_rows)
        mean_loss = (loss_sum / (micro_count * micro_tokens)).reshape(1)
        return mean_loss, acc_first[None], acc_second[None], grad_head + grad_lookup

    return jax.shard_map(
        stage_body,
        mesh=mesh,
        in_specs=(P("dp", None), P("dp", None), P("stage", None), P("stage", None, None), P("stage", None, None)),
        out_specs=(P("dp"), P(("dp", "stage"), None, None), P(("dp", "stage"), None, None), P(("dp", "stage"), None)),
        check_vma=False,
    )
```

profile of v0, /device:TPU:122, one launch (start us, length us, event | category | flops | bytes accessed | tf_op | source)
XLA Modules:
  0.0 1835.8 jit_solution(16177014126310966604)
XLA Ops:
  25.0 61.6 %all-reduce.5.cloned.1.call-done = bf16[8,256,768]{2,1,0:T(8,128)(2,1)} async-done(((bf16[8,256,768]{2,1,0:T(8,128)(2,1)}), bf16[8,256,768]{2,1,0:T(8,128)(2,1)}) %all-reduce.5.cloned.1.call-update) | async-done | bytes 3145744 | tf_op jit(solution)/shard_map/psum | solution.py:61
  89.5 255.3 %while.53 = (s32[]{:T(128)}, bf16[256,768]{1,0:T(8,128)(2,1)}, bf16[8,256,768]{2,1,0:T(8,128)(2,1)}, bf16[8,256,768]{2,1,0:T(8,128)(2,1)S(1)}, s32[]{:T(128)}, /...) while((s32[]{:T(128)}, bf16[256,768]{1,0:T(8,128)(2,1)}, ...), condition=%wide.region_4.5_spmd, body=%wide.region_1.4_spmd.sunk | while | flops 2424176640 | bytes 17302292 | solution.py:76
  350.2 75.9 %all-reduce.7.cloned.1.call-done = bf16[8,256,768]{2,1,0:T(8,128)(2,1)} async-done(((bf16[8,256,768]{2,1,0:T(8,128)(2,1)}), bf16[8,256,768]{2,1,0:T(8,128)(2,1)}) %all-reduce.7.cloned.1.call-update) | async-done | bytes 3145744 | tf_op jit(solution)/shard_map/psum | solution.py:79
  426.1 848.3 %while.55 = (s32[]{:T(128)}, f32[6288,768]{1,0:T(8,128)}, f32[]{:T(128)}, f32[8,256,768]{2,1,0:T(8,128)}, bf16[8,256,768]{2,1,0:T(8,128)(2,1)}, /*index=5*/bf16[...) while((s32[]{:T(128)}, f32[6288,768]{1,0:T(8,128)}, f32[]{:T(128)}, ...), condition=%wide.region_15.16_spmd.clone, body=%wide.region_7.15_spmd.clone.sunk | while | flops 7461286912 | bytes 91601088 | solution.py:98
  490.9 40.0 %all-reduce.11.cloned.1.call-done = f32[1,256,768]{2,1,0:T(8,128)} async-done(((f32[1,256,768]{2,1,0:T(8,128)}), f32[1,256,768]{2,1,0:T(8,128)}) %all-reduce.11.cloned.1.call-update) | async-done | bytes 786448 | tf_op jit(solution)/shard_map/while/body/eval_jaxpr/psum | solution.py:93
  581.6 19.5 %select_add_fusion.2 = f32[6288,768]{1,0:T(8,128)} fusion(f32[6288,768]{1,0:T(8,128)} %get-tuple-element.875, pred[]{:T(512)S(6)} %compare.3, bf16[8,256,768]{2,1,0:T(8,128)(2,1)} %get-tuple-element.887, s32[]{:T(128)S(6)} %copy.42, f32[256,6288]{0,1:T(8,128)} %get-tuple-element.814, f32[256]{0:T(256)S(1)} %bitcast.114, s32[256]{0:T(256)S(1)} %bitcast.118, ...), kind=kOutput, calls=%fused_computation.63.clone.1 | convolution fusion | flops 2493468672 | bytes 45468676 | tf_op jit(solution)/shard_map/while/body/eval_jaxpr/tv,td->vd/dot_general | solution.py:94
  602.4 34.4 %all-reduce.11.cloned.1.call-done = f32[1,256,768]{2,1,0:T(8,128)} async-done(((f32[1,256,768]{2,1,0:T(8,128)}), f32[1,256,768]{2,1,0:T(8,128)}) %all-reduce.11.cloned.1.call-update) | async-done | bytes 786448 | tf_op jit(solution)/shard_map/while/body/eval_jaxpr/psum | solution.py:93
  687.5 19.5 %select_add_fusion.2 = f32[6288,768]{1,0:T(8,128)} fusion(f32[6288,768]{1,0:T(8,128)} %get-tuple-element.875, pred[]{:T(512)S(6)} %compare.3, bf16[8,256,768]{2,1,0:T(8,128)(2,1)} %get-tuple-element.887, s32[]{:T(128)S(6)} %copy.42, f32[256,6288]{0,1:T(8,128)} %get-tuple-element.814, f32[256]{0:T(256)S(1)} %bitcast.114, s32[256]{0:T(256)S(1)} %bitcast.118, ...), kind=kOutput, calls=%fused_computation.63.clone.1 | convolution fusion | flops 2493468672 | bytes 45468676 | tf_op jit(solution)/shard_map/while/body/eval_jaxpr/tv,td->vd/dot_general | solution.py:94
  708.3 34.4 %all-reduce.11.cloned.1.call-done = f32[1,256,768]{2,1,0:T(8,128)} async-done(((f32[1,256,768]{2,1,0:T(8,128)}), f32[1,256,768]{2,1,0:T(8,128)}) %all-reduce.11.cloned.1.call-update) | async-done | bytes 786448 | tf_op jit(solution)/shard_map/while/body/eval_jaxpr/psum | solution.py:93
  793.4 19.5 %select_add_fusion.2 = f32[6288,768]{1,0:T(8,128)} fusion(f32[6288,768]{1,0:T(8,128)} %get-tuple-element.875, pred[]{:T(512)S(6)} %compare.3, bf16[8,256,768]{2,1,0:T(8,128)(2,1)} %get-tuple-element.887, s32[]{:T(128)S(6)} %copy.42, f32[256,6288]{0,1:T(8,128)} %get-tuple-element.814, f32[256]{0:T(256)S(1)} %bitcast.114, s32[256]{0:T(256)S(1)} %bitcast.118, ...), kind=kOutput, calls=%fused_computation.63.clone.1 | convolution fusion | flops 2493468672 | bytes 45468676 | tf_op jit(solution)/shard_map/while/body/eval_jaxpr/tv,td->vd/dot_general | solution.py:94
  814.2 34.4 %all-reduce.11.cloned.1.call-done = f32[1,256,768]{2,1,0:T(8,128)} async-done(((f32[1,256,768]{2,1,0:T(8,128)}), f32[1,256,768]{2,1,0:T(8,128)}) %all-reduce.11.cloned.1.call-update) | async-done | bytes 786448 | tf_op jit(solution)/shard_map/while/body/eval_jaxpr/psum | solution.py:93
  899.3 19.5 %select_add_fusion.2 = f32[6288,768]{1,0:T(8,128)} fusion(f32[6288,768]{1,0:T(8,128)} %get-tuple-element.875, pred[]{:T(512)S(6)} %compare.3, bf16[8,256,768]{2,1,0:T(8,128)(2,1)} %get-tuple-element.887, s32[]{:T(128)S(6)} %copy.42, f32[256,6288]{0,1:T(8,128)} %get-tuple-element.814, f32[256]{0:T(256)S(1)} %bitcast.114, s32[256]{0:T(256)S(1)} %bitcast.118, ...), kind=kOutput, calls=%fused_computation.63.clone.1 | convolution fusion | flops 2493468672 | bytes 45468676 | tf_op jit(solution)/shard_map/while/body/eval_jaxpr/tv,td->vd/dot_general | solution.py:94
  920.1 34.4 %all-reduce.11.cloned.1.call-done = f32[1,256,768]{2,1,0:T(8,128)} async-done(((f32[1,256,768]{2,1,0:T(8,128)}), f32[1,256,768]{2,1,0:T(8,128)}) %all-reduce.11.cloned.1.call-update) | async-done | bytes 786448 | tf_op jit(solution)/shard_map/while/body/eval_jaxpr/psum | solution.py:93
  1005.2 19.5 %select_add_fusion.2 = f32[6288,768]{1,0:T(8,128)} fusion(f32[6288,768]{1,0:T(8,128)} %get-tuple-element.875, pred[]{:T(512)S(6)} %compare.3, bf16[8,256,768]{2,1,0:T(8,128)(2,1)} %get-tuple-element.887, s32[]{:T(128)S(6)} %copy.42, f32[256,6288]{0,1:T(8,128)} %get-tuple-element.814, f32[256]{0:T(256)S(1)} %bitcast.114, s32[256]{0:T(256)S(1)} %bitcast.118, ...), kind=kOutput, calls=%fused_computation.63.clone.1 | convolution fusion | flops 2493468672 | bytes 45468676 | tf_op jit(solution)/shard_map/while/body/eval_jaxpr/tv,td->vd/dot_general | solution.py:94
  1026.0 34.4 %all-reduce.11.cloned.1.call-done = f32[1,256,768]{2,1,0:T(8,128)} async-done(((f32[1,256,768]{2,1,0:T(8,128)}), f32[1,256,768]{2,1,0:T(8,128)}) %all-reduce.11.cloned.1.call-update) | async-done | bytes 786448 | tf_op jit(solution)/shard_map/while/body/eval_jaxpr/psum | solution.py:93
  1111.2 19.5 %select_add_fusion.2 = f32[6288,768]{1,0:T(8,128)} fusion(f32[6288,768]{1,0:T(8,128)} %get-tuple-element.875, pred[]{:T(512)S(6)} %compare.3, bf16[8,256,768]{2,1,0:T(8,128)(2,1)} %get-tuple-element.887, s32[]{:T(128)S(6)} %copy.42, f32[256,6288]{0,1:T(8,128)} %get-tuple-element.814, f32[256]{0:T(256)S(1)} %bitcast.114, s32[256]{0:T(256)S(1)} %bitcast.118, ...), kind=kOutput, calls=%fused_computation.63.clone.1 | convolution fusion | flops 2493468672 | bytes 45468676 | tf_op jit(solution)/shard_map/while/body/eval_jaxpr/tv,td->vd/dot_general | solution.py:94
  1132.0 34.4 %all-reduce.11.cloned.1.call-done = f32[1,256,768]{2,1,0:T(8,128)} async-done(((f32[1,256,768]{2,1,0:T(8,128)}), f32[1,256,768]{2,1,0:T(8,128)}) %all-reduce.11.cloned.1.call-update) | async-done | bytes 786448 | tf_op jit(solution)/shard_map/while/body/eval_jaxpr/psum | solution.py:93
  1217.2 19.5 %select_add_fusion.2 = f32[6288,768]{1,0:T(8,128)} fusion(f32[6288,768]{1,0:T(8,128)} %get-tuple-element.875, pred[]{:T(512)S(6)} %compare.3, bf16[8,256,768]{2,1,0:T(8,128)(2,1)} %get-tuple-element.887, s32[]{:T(128)S(6)} %copy.42, f32[256,6288]{0,1:T(8,128)} %get-tuple-element.814, f32[256]{0:T(256)S(1)} %bitcast.114, s32[256]{0:T(256)S(1)} %bitcast.118, ...), kind=kOutput, calls=%fused_computation.63.clone.1 | convolution fusion | flops 2493468672 | bytes 45468676 | tf_op jit(solution)/shard_map/while/body/eval_jaxpr/tv,td->vd/dot_general | solution.py:94
  1237.9 34.4 %all-reduce.11.cloned.1.call-done = f32[1,256,768]{2,1,0:T(8,128)} async-done(((f32[1,256,768]{2,1,0:T(8,128)}), f32[1,256,768]{2,1,0:T(8,128)}) %all-reduce.11.cloned.1.call-update) | async-done | bytes 786448 | tf_op jit(solution)/shard_map/while/body/eval_jaxpr/psum | solution.py:93
  1292.7 432.7 %while.54 = (s32[]{:T(128)}, bf16[256,768]{1,0:T(8,128)(2,1)S(1)}, f32[768,3072]{1,0:T(8,128)}, f32[3072,768]{1,0:T(8,128)}, bf16[8,256,768]{2,1,0:T(8,128)(2,1)...) while((s32[]{:T(128)}, bf16[256,768]{1,0:T(8,128)(2,1)S(1)}, ...), condition=%wide.region_20.21_spmd, body=%wide.region_17.20_spmd.sunk | while | flops 6068305920 | bytes 222562448 | solution.py:120
  1338.8 93.7 %collective-permute-done.1 = bf16[256,768]{1,0:T(8,128)(2,1)S(1)} collective-permute-done((bf16[256,768]{1,0:T(8,128)(2,1)S(1)}, bf16[256,768]{1,0:T(8,128)(2,1)S(1)}, u32[]{:S(2)}, u32[]{:S(2)}) %collective-permute-start.1) | collective-permute-done | bytes 393248 | tf_op jit(solution)/shard_map/while/body/eval_jaxpr/ppermute | solution.py:117
  1433.5 21.5 %conditional.5 = (bf16[256,768]{1,0:T(8,128)(2,1)S(1)}, f32[768,3072]{1,0:T(8,128)}, f32[3072,768]{1,0:T(8,128)}) conditional(s32[]{:T(128)} %convert_element_type.126, (bf16[256,768]{1,0:T(8,128)(2,1)S(1)}, f32[768,3072]{1,0:T(8,128)}, f32[3072,768]{1,0:T(8,128)}) %tuple.113, (bf16[256,768]{1,0:T(8,128)(2,1)S(1)}, bf16[3072,768]{1,0:T(8,128)(2,1)}, ...), branch_computations={%region_18.18_spmd, %region_19.19_spmd} | conditional | flops 6067912704 | bytes 217843008 | solution.py:115
  1465.1 21.5 %conditional.5 = (bf16[256,768]{1,0:T(8,128)(2,1)S(1)}, f32[768,3072]{1,0:T(8,128)}, f32[3072,768]{1,0:T(8,128)}) conditional(s32[]{:T(128)} %convert_element_type.126, (bf16[256,768]{1,0:T(8,128)(2,1)S(1)}, f32[768,3072]{1,0:T(8,128)}, f32[3072,768]{1,0:T(8,128)}) %tuple.113, (bf16[256,768]{1,0:T(8,128)(2,1)S(1)}, bf16[3072,768]{1,0:T(8,128)(2,1)}, ...), branch_computations={%region_18.18_spmd, %region_19.19_spmd} | conditional | flops 6067912704 | bytes 217843008 | solution.py:115
  1496.8 21.5 %conditional.5 = (bf16[256,768]{1,0:T(8,128)(2,1)S(1)}, f32[768,3072]{1,0:T(8,128)}, f32[3072,768]{1,0:T(8,128)}) conditional(s32[]{:T(128)} %convert_element_type.126, (bf16[256,768]{1,0:T(8,128)(2,1)S(1)}, f32[768,3072]{1,0:T(8,128)}, f32[3072,768]{1,0:T(8,128)}) %tuple.113, (bf16[256,768]{1,0:T(8,128)(2,1)S(1)}, bf16[3072,768]{1,0:T(8,128)(2,1)}, ...), branch_computations={%region_18.18_spmd, %region_19.19_spmd} | conditional | flops 6067912704 | bytes 217843008 | solution.py:115
  1528.4 21.5 %conditional.5 = (bf16[256,768]{1,0:T(8,128)(2,1)S(1)}, f32[768,3072]{1,0:T(8,128)}, f32[3072,768]{1,0:T(8,128)}) conditional(s32[]{:T(128)} %convert_element_type.126, (bf16[256,768]{1,0:T(8,128)(2,1)S(1)}, f32[768,3072]{1,0:T(8,128)}, f32[3072,768]{1,0:T(8,128)}) %tuple.113, (bf16[256,768]{1,0:T(8,128)(2,1)S(1)}, bf16[3072,768]{1,0:T(8,128)(2,1)}, ...), branch_computations={%region_18.18_spmd, %region_19.19_spmd} | conditional | flops 6067912704 | bytes 217843008 | solution.py:115
  1560.0 21.5 %conditional.5 = (bf16[256,768]{1,0:T(8,128)(2,1)S(1)}, f32[768,3072]{1,0:T(8,128)}, f32[3072,768]{1,0:T(8,128)}) conditional(s32[]{:T(128)} %convert_element_type.126, (bf16[256,768]{1,0:T(8,128)(2,1)S(1)}, f32[768,3072]{1,0:T(8,128)}, f32[3072,768]{1,0:T(8,128)}) %tuple.113, (bf16[256,768]{1,0:T(8,128)(2,1)S(1)}, bf16[3072,768]{1,0:T(8,128)(2,1)}, ...), branch_computations={%region_18.18_spmd, %region_19.19_spmd} | conditional | flops 6067912704 | bytes 217843008 | solution.py:115
  1591.6 21.5 %conditional.5 = (bf16[256,768]{1,0:T(8,128)(2,1)S(1)}, f32[768,3072]{1,0:T(8,128)}, f32[3072,768]{1,0:T(8,128)}) conditional(s32[]{:T(128)} %convert_element_type.126, (bf16[256,768]{1,0:T(8,128)(2,1)S(1)}, f32[768,3072]{1,0:T(8,128)}, f32[3072,768]{1,0:T(8,128)}) %tuple.113, (bf16[256,768]{1,0:T(8,128)(2,1)S(1)}, bf16[3072,768]{1,0:T(8,128)(2,1)}, ...), branch_computations={%region_18.18_spmd, %region_19.19_spmd} | conditional | flops 6067912704 | bytes 217843008 | solution.py:115
  1623.3 21.5 %conditional.5 = (bf16[256,768]{1,0:T(8,128)(2,1)S(1)}, f32[768,3072]{1,0:T(8,128)}, f32[3072,768]{1,0:T(8,128)}) conditional(s32[]{:T(128)} %convert_element_type.126, (bf16[256,768]{1,0:T(8,128)(2,1)S(1)}, f32[768,3072]{1,0:T(8,128)}, f32[3072,768]{1,0:T(8,128)}) %tuple.113, (bf16[256,768]{1,0:T(8,128)(2,1)S(1)}, bf16[3072,768]{1,0:T(8,128)(2,1)}, ...), branch_computations={%region_18.18_spmd, %region_19.19_spmd} | conditional | flops 6067912704 | bytes 217843008 | solution.py:115
  1654.9 21.5 %conditional.5 = (bf16[256,768]{1,0:T(8,128)(2,1)S(1)}, f32[768,3072]{1,0:T(8,128)}, f32[3072,768]{1,0:T(8,128)}) conditional(s32[]{:T(128)} %convert_element_type.126, (bf16[256,768]{1,0:T(8,128)(2,1)S(1)}, f32[768,3072]{1,0:T(8,128)}, f32[3072,768]{1,0:T(8,128)}) %tuple.113, (bf16[256,768]{1,0:T(8,128)(2,1)S(1)}, bf16[3072,768]{1,0:T(8,128)(2,1)}, ...), branch_computations={%region_18.18_spmd, %region_19.19_spmd} | conditional | flops 6067912704 | bytes 217843008 | solution.py:115
  1684.7 25.2 %collective-permute-start.1 = (bf16[256,768]{1,0:T(8,128)(2,1)S(1)}, bf16[256,768]{1,0:T(8,128)(2,1)S(1)}, u32[]{:S(2)}, u32[]{:S(2)}) collective-permute-start(bf16[256,768]{1,0:T(8,128)(2,1)S(1)} %get-tuple-element.804), channel_id=1, source_target_pairs={{1,0},{2,1},{3,2},{4,3},{5,4},{6,5},{7,6},{9,8},{10,9},{11,10},{12... | collective-permute-start | bytes 1179656 | tf_op jit(solution)/shard_map/while/body/eval_jaxpr/ppermute | solution.py:117
  1728.0 72.1 %all-reduce.9.cloned.1.call-done = bf16[2048,768]{1,0:T(8,128)(2,1)} async-done(((bf16[2048,768]{1,0:T(8,128)(2,1)}), bf16[2048,768]{1,0:T(8,128)(2,1)}) %all-reduce.9.cloned.1.call-update) | async-done | bytes 3145744 | tf_op jit(solution)/shard_map/psum | solution.py:122
  1800.0 28.1 %scatter_custom_fusion = f32[6288,768]{1,0:T(8,128)} fusion(f32[6288,768]{1,0:T(8,128)} %get-tuple-element.537, s32[2048]{0:T(1024)S(1)} %bitcast.122, bf16[2048,768]{1,0:T(8,128)(2,1)} %all-reduce.9.cloned.1.call-done), kind=kCustom, calls=%fused_computation.94 | custom fusion | flops 3145728 | bytes 22462464 | tf_op jit(solution)/shard_map/scatter-add | solution.py:124
  (577 shorter events, 1099.8 us)
Async XLA Ops:
  7.2 79.4 %all-reduce.5.cloned.1.call-start = ((), (), s32[]{:S(2)}) async-start(), calls=%async_computation | async-start | bytes 6291456 | tf_op jit(solution)/shard_map/psum | solution.py:61
  24.9 401.2 %all-reduce.7.cloned.1.call-start = ((), (), s32[]{:S(2)}) async-start(), calls=%async_computation.1 | async-start | bytes 6291456 | tf_op jit(solution)/shard_map/psum | solution.py:79
  104.8 19.1 %collective-permute-start = (bf16[256,768]{1,0:T(8,128)(2,1)S(1)}, bf16[256,768]{1,0:T(8,128)(2,1)}, u32[]{:S(2)}, u32[]{:S(2)}) collective-permute-start(bf16[256,768]{1,0:T(8,128)(2,1)S(1)} %get-tuple-element.937), channel_id=1, source_target_pairs={{0,1},{1,2},{2,3},{3,4},{4,5},{5,6},{6,7},{8,9},{9,10},{10,11},{11... | collective-permute-start | bytes 1179656 | tf_op jit(solution)/shard_map/while/body/eval_jaxpr/ppermute | solution.py:74
  134.6 9.1 collective-permute-start
  154.4 9.1 collective-permute-start
  174.2 9.1 collective-permute-start
  194.0 9.1 collective-permute-start
  213.8 9.1 collective-permute-start
  233.6 9.1 collective-permute-start
  253.5 9.1 collective-permute-start
  273.3 9.1 collective-permute-start
  309.9 10.6 collective-permute-start
  426.1 104.8 %all-reduce.11.cloned.1.call-start = ((), (), s32[]{:S(2)}) async-start(), calls=%async_computation.3 | async-start | bytes 1572864 | tf_op jit(solution)/shard_map/while/body/eval_jaxpr/psum | solution.py:93
  532.9 103.8 %all-reduce.11.cloned.1.call-start = ((), (), s32[]{:S(2)}) async-start(), calls=%async_computation.3 | async-start | bytes 1572864 | tf_op jit(solution)/shard_map/while/body/eval_jaxpr/psum | solution.py:93
  638.8 103.8 %all-reduce.11.cloned.1.call-start = ((), (), s32[]{:S(2)}) async-start(), calls=%async_computation.3 | async-start | bytes 1572864 | tf_op jit(solution)/shard_map/while/body/eval_jaxpr/psum | solution.py:93
  744.8 103.8 %all-reduce.11.cloned.1.call-start = ((), (), s32[]{:S(2)}) async-start(), calls=%async_computation.3 | async-start | bytes 1572864 | tf_op jit(solution)/shard_map/while/body/eval_jaxpr/psum | solution.py:93
  850.7 103.8 %all-reduce.11.cloned.1.call-start = ((), (), s32[]{:S(2)}) async-start(), calls=%async_computation.3 | async-start | bytes 1572864 | tf_op jit(solution)/shard_map/while/body/eval_jaxpr/psum | solution.py:93
  956.6 103.9 %all-reduce.11.cloned.1.call-start = ((), (), s32[]{:S(2)}) async-start(), calls=%async_computation.3 | async-start | bytes 1572864 | tf_op jit(solution)/shard_map/while/body/eval_jaxpr/psum | solution.py:93
  1062.5 103.9 %all-reduce.11.cloned.1.call-start = ((), (), s32[]{:S(2)}) async-start(), calls=%async_computation.3 | async-start | bytes 1572864 | tf_op jit(solution)/shard_map/while/body/eval_jaxpr/psum | solution.py:93
  1168.5 103.9 %all-reduce.11.cloned.1.call-start = ((), (), s32[]{:S(2)}) async-start(), calls=%async_computation.3 | async-start | bytes 1572864 | tf_op jit(solution)/shard_map/while/body/eval_jaxpr/psum | solution.py:93
  1274.4 525.6 %all-reduce.9.cloned.1.call-start = ((), (), s32[]{:S(2)}) async-start(), calls=%async_computation.2 | async-start | bytes 6291456 | tf_op jit(solution)/shard_map/psum | solution.py:122
  1302.3 9.1 collective-permute-start.1
  1312.5 9.1 collective-permute-start.1
  1322.7 9.1 collective-permute-start.1
  1333.0 99.5 %collective-permute-start.1 = (bf16[256,768]{1,0:T(8,128)(2,1)S(1)}, bf16[256,768]{1,0:T(8,128)(2,1)S(1)}, u32[]{:S(2)}, u32[]{:S(2)}) collective-permute-start(bf16[256,768]{1,0:T(8,128)(2,1)S(1)} %get-tuple-element.804), channel_id=1, source_target_pairs={{1,0},{2,1},{3,2},{4,3},{5,4},{6,5},{7,6},{9,8},{10,9},{11,10},{12... | collective-permute-start | bytes 1179656 | tf_op jit(solution)/shard_map/while/body/eval_jaxpr/ppermute | solution.py:117
  1455.0 9.1 collective-permute-start.1
  1486.6 9.1 collective-permute-start.1
  1518.2 9.1 collective-permute-start.1
  1549.9 9.1 collective-permute-start.1
  1581.5 9.1 collective-permute-start.1
  1684.7 30.5 %collective-permute-start.1 = (bf16[256,768]{1,0:T(8,128)(2,1)S(1)}, bf16[256,768]{1,0:T(8,128)(2,1)S(1)}, u32[]{:S(2)}, u32[]{:S(2)}) collective-permute-start(bf16[256,768]{1,0:T(8,128)(2,1)S(1)} %get-tuple-element.804), channel_id=1, source_target_pairs={{1,0},{2,1},{3,2},{4,3},{5,4},{6,5},{7,6},{9,8},{10,9},{11,10},{12... | collective-permute-start | bytes 1179656 | tf_op jit(solution)/shard_map/while/body/eval_jaxpr/ppermute | solution.py:117
  1716.3 9.1 collective-permute-start.1
  (98 other events, 1395.0 us)
Sparse Core Ops, SparseCore 0:
  25.0 61.5 all-reduce.4
  349.7 76.3 all-reduce.6
  475.8 55.0 all-reduce.10
  581.7 55.0 all-reduce.10
  687.6 55.0 all-reduce.10
  793.5 55.0 all-reduce.10
  899.4 55.0 all-reduce.10
  1005.3 55.0 all-reduce.10
  1111.3 55.0 all-reduce.10
  1217.3 55.0 all-reduce.10
  1727.5 72.5 all-reduce.8
where the time goes:
time: 1840 us
  waiting for transfers between devices  740 us (40%)
  matrix products  492 us (27%)
  blocking collectives  202 us (11%)
  other arithmetic  145 us (8%)
  local copies, waits for them, and re-layouts  120 us (7%)
  starting transfers between devices  113 us (6%)
    psum x8, waiting for transfers between devices, head_step(): lax.psum(jnp.einsum('tv,vd->td', grad_logits, emb_rows, preferred_element...  281 us
    ppermute x15, waiting for transfers between devices, bwd_tick(): lax.ppermute(grad_in, 'stage', bwd_pairs)  154 us
    dot_general x8, matrix products, head_step(): jnp.einsum('tv,td->vd', grad_logits, normed_mb, preferred_element_type=jn...  151 us
    pmax x8, blocking collectives, head_step(): row_max = lax.pmax(jnp.max(logits, axis=1), 'stage')  102 us
    psum x8, blocking collectives, head_step(): lax.psum(jnp.stack([jnp.sum(exp_logits, axis=1), jnp.sum(jnp.where(is_lab...  100 us
    ppermute x15, waiting for transfers between devices, fwd_tick(): return (lax.ppermute(act_out, 'stage', fwd_pairs), saved_in, last_out)  95.5 us
    dot_general x8, matrix products, head_step(): jnp.einsum('tv,vd->td', grad_logits, emb_rows, preferred_element_type=jnp...  76.6 us
    psum x1, waiting for transfers between devices, stage_body(): lax.psum(jnp.where(is_last, normed_f.astype(jnp.bfloat16), 0), 'stage')  75.9 us
  transfers between devices with their start and end apart: 41, of which 41 were waited for; matrix products, arithmetic and copies ran while one was open for 10% of the time, Pallas kernels for 0%

commit v1 on v0

v1 whole, which is shorter than its diff:
```python
import functools
import math

import jax
import jax.numpy as jnp
from jax import lax
from jax.experimental import pallas as pl
from jax.experimental.pallas import tpu as pltpu
from jax.sharding import PartitionSpec as P

NORM_EPS = 1e-6
MESH = pl.DeviceIdType.MESH
F32 = jnp.float32
BF16 = jnp.bfloat16
GELU_A = math.sqrt(2.0 / math.pi)
GELU_B = 0.044715
LOG2E = math.log2(math.e)
CHUNK = 128
HEAD_MBS = 2
VMEM_LIMIT = 67_000_000


def dot_nn(a, b):
    return lax.dot_general(a, b, (((1,), (0,)), ((), ())), preferred_element_type=F32)


def dot_nt(a, b):
    return lax.dot_general(a, b, (((1,), (1,)), ((), ())), preferred_element_type=F32)


def dot_tn(a, b):
    return lax.dot_general(a, b, (((0,), (0,)), ((), ())), preferred_element_type=F32)


def gelu_f32(pre):
    inner = GELU_A * (pre + GELU_B * (pre * pre * pre))
    return (0.5 * pre) * (1.0 + jnp.tanh(inner))


def norm_scale(x_f32):
    return lax.rsqrt(jnp.mean(x_f32 * x_f32, axis=-1, keepdims=True) + NORM_EPS)


def remote(src, dst, send_sem, recv_sem, stage):
    return pltpu.make_async_remote_copy(
        src_ref=src, dst_ref=dst, send_sem=send_sem, recv_sem=recv_sem, device_id={"stage": stage}, device_id_type=MESH
    )


def group_barrier(stage, n_stage):
    barrier = pltpu.get_barrier_semaphore()
    for off in range(1, n_stage):
        pl.semaphore_signal(barrier, inc=1, device_id={"stage": lax.rem(stage + off, n_stage)}, device_id_type=MESH)
    pl.semaphore_wait(barrier, n_stage - 1)


def vocab_tile(rows):
    for parts in range(2, rows + 1):
        if rows % parts == 0 and (rows // parts) % 16 == 0 and rows // parts <= 2400:
            return rows // parts
    return rows


def sub_blocks(rows, size):
    return [(start, min(size, rows - start)) for start in range(0, rows, size)]


def forward_chunk(x, w1, w2, pre_slot, hid):
    ffn = w1.shape[1]
    width = ffn // 4
    for part in range(4):
        cols = pl.ds(part * width, width)
        pre = dot_nn(x, w1[:, cols])
        pre_slot[:, cols] = pre
        hid[:, cols] = gelu_f32(pre).astype(BF16)
    return x.astype(F32) + dot_nn(hid[...], w2[...])


def head_logits(n_t, emb, logits, lab_row, tokens):
    rows = emb.shape[0]
    tile = vocab_tile(rows)
    c2 = LOG2E * emb.shape[1] ** -0.5

    def tile_step(idx, carry):
        mx, sm, lb = carry
        base = pl.multiple_of(idx * tile, 16)
        for start, size in sub_blocks(tile, 256):
            at = pl.ds(base + start, size)
            block = dot_nn(emb[at, :], n_t[...])
            logits[at, :] = block
            b3 = block.reshape(size // 8, 8, tokens)
            row_ids = lax.broadcasted_iota(jnp.int32, (size, tokens), 0) + (base + start)
            hit = jnp.where(row_ids == lab_row, block, 0.0).reshape(size // 8, 8, tokens)
            mx_new = jnp.maximum(mx, jnp.max(b3, axis=0))
            sm = sm * jnp.exp2((mx - mx_new) * c2) + jnp.sum(jnp.exp2((b3 - mx_new[None]) * c2), axis=0)
            lb = lb + jnp.sum(hit, axis=0)
            mx = mx_new
        return mx, sm, lb

    init = (jnp.full((8, tokens), -3.0e38, F32), jnp.zeros((8, tokens), F32), jnp.zeros((8, tokens), F32))
    mx, sm, lb = lax.fori_loop(0, rows // tile, tile_step, init)
    top = jnp.max(mx, axis=0, keepdims=True)
    tot = jnp.sum(sm * jnp.exp2((mx - top) * c2), axis=0, keepdims=True)
    lab = jnp.sum(lb, axis=0, keepdims=True)
    return top, tot, lab


def head_grad_tile(idx, tile, emb, logits, d_slot, lab_row, top, shift, tokens):
    scale = emb.shape[1] ** -0.5
    c2 = LOG2E * scale
    base = pl.multiple_of(idx * tile, 16)
    for start, size in sub_blocks(tile, 256):
        at = pl.ds(base + start, size)
        row_ids = lax.broadcasted_iota(jnp.int32, (size, tokens), 0) + (base + start)
        prob = jnp.exp2((logits[at, :] - top) * c2 - shift)
        d_slot[pl.ds(start, size), :] = (prob - jnp.where(row_ids == lab_row, scale, 0.0)).astype(BF16)
    return dot_tn(d_slot[...], emb[pl.ds(base, tile), :])


def forward_head_kernel(
    n_stage, lab_ref, part_hbm, emb_hbm, w1_hbm, w2_hbm,
    pre_out, xin_out, n_out, dt_out, dxl_out, loss_out,
    emb, w1, w2, x_in, x_out, n_all, comb, buf_a, buf_b, logits, n_t, pre_stg, hid, d_stg, gn_acc, stats, loss_acc,
    load_sem, part_sem, lk_send, lk_a, lk_b, x_send, x_recv, n_send, n_recv, st_send, st_recv,
    g_send, g_a, g_b, pre_sem, d_sem, out_sem,
):
    s = lax.axis_index("stage")
    last = n_stage - 1
    mbs, mtok, dim = x_in.shape
    n_half = mtok // CHUNK
    rows = emb.shape[0]
    tile = vocab_tile(rows)
    tokens = HEAD_MBS * mtok
    rounds = mbs // HEAD_MBS
    scale = dim ** -0.5
    c2 = LOG2E * scale
    row_start = s * rows

    loads = [pltpu.make_async_copy(src, dst, load_sem.at[i])
             for i, (src, dst) in enumerate([(w1_hbm, w1), (w2_hbm, w2), (emb_hbm, emb)])]
    for mb in range(mbs):
        pltpu.make_async_copy(part_hbm.at[mb], comb.at[mb], part_sem.at[mb]).start()
    for ld in loads:
        ld.start()
    group_barrier(s, n_stage)

    def half(mb, hf):
        return (mb, pl.ds(pl.multiple_of(hf * CHUNK, CHUNK), CHUNK))

    def at_half(ref, mb, hf):
        return ref.at[mb, pl.ds(pl.multiple_of(hf * CHUNK, CHUNK), CHUNK)]

    def lk_copy(mb, hf, child):
        parent, slot, sem = {1: (0, buf_a, lk_a), 2: (3, buf_a, lk_a), 3: (1, buf_a, lk_a), 4: (5, buf_a, lk_a),
                             6: (7, buf_a, lk_a), 5: (3, buf_b, lk_b), 7: (0, buf_b, lk_b)}[child]
        c = mb * n_half + hf
        return remote(at_half(comb, mb, hf), at_half(slot, mb, hf), lk_send.at[c], sem.at[c], parent)

    def lk_wait(mb, hf, slot, sem):
        c = mb * n_half + hf
        remote(at_half(comb, mb, hf), at_half(slot, mb, hf), lk_send.at[c], sem.at[c], 0).wait_recv()

    def chunks(fn):
        def step(c, _):
            fn(c // n_half, lax.rem(c, n_half))
            return 0
        lax.fori_loop(0, mbs * n_half, step, 0)

    def halves(mb, fn):
        def step(hf, _):
            fn(mb, hf)
            return 0
        lax.fori_loop(0, n_half, step, 0)

    def part_wait(mb, _):
        pltpu.make_async_copy(part_hbm.at[mb], comb.at[mb], part_sem.at[mb]).wait()
        return 0

    lax.fori_loop(0, mbs, part_wait, 0)

    for child in (2, 4, 6):
        @pl.when(s == child)
        def _(child=child):
            chunks(lambda mb, hf: lk_copy(mb, hf, child).start())

    def add_in(mb, hf, slots):
        idx = half(mb, hf)
        total = comb[idx].astype(F32)
        for slot, sem in slots:
            lk_wait(mb, hf, slot, sem)
            total = total + slot[idx].astype(F32)
        comb[idx] = total.astype(BF16)

    for child in (5, 7):
        @pl.when(s == child)
        def _(child=child):
            def fwd(mb, hf):
                add_in(mb, hf, [(buf_a, lk_a)])
                lk_copy(mb, hf, child).start()
            chunks(fwd)

    loads[0].wait()
    loads[1].wait()
    loads[2].wait()

    def x_copy(mb, hf, dst_stage):
        c = mb * n_half + hf
        return remote(at_half(x_out, mb, hf), at_half(x_in, mb, hf), x_send.at[c], x_recv.at[c], dst_stage)

    def n_copy(mb, hf, lane, dst_stage):
        c = mb * n_half + hf
        return remote(at_half(n_all, mb, hf), at_half(n_all, mb, hf), n_send.at[lane, c], n_recv.at[c], dst_stage)

    def pre_copy(c):
        slot = lax.rem(c, 2)
        return pltpu.make_async_copy(pre_stg.at[slot], pre_out.at[c], pre_sem.at[slot])

    def fwd_chunk(mb, hf):
        c = mb * n_half + hf
        idx = half(mb, hf)

        @pl.when(s == 0)
        def _():
            total = comb[idx].astype(F32)
            for slot, sem in ((buf_a, lk_a), (buf_b, lk_b)):
                lk_wait(mb, hf, slot, sem)
                total = total + slot[idx].astype(F32)
            x_in[idx] = total.astype(BF16)

        @pl.when(s > 0)
        def _():
            x_copy(mb, hf, 0).wait_recv()

        @pl.when(c >= 2)
        def _():
            pre_copy(c - 2).wait()

        out = forward_chunk(x_in[idx], w1, w2, pre_stg.at[lax.rem(c, 2)], hid).astype(BF16)
        x_out[idx] = out
        pre_copy(c).start()

        @pl.when(s < last)
        def _():
            x_copy(mb, hf, s + 1).start()

        @pl.when(s == last)
        def _():
            out_f = out.astype(F32)
            n_all[idx] = (out_f * norm_scale(out_f)).astype(BF16)
            for lane, dst in enumerate((5, 1, 6)):
                n_copy(mb, hf, lane, dst).start()

    def n_forward(mb, hf):
        @pl.when(s < last)
        def _():
            n_copy(mb, hf, 0, last).wait_recv()
        for src, dsts in ((5, (3, 4)), (3, (2,)), (1, (0,))):
            @pl.when(s == src)
            def _(dsts=dsts):
                for lane, dst in enumerate(dsts):
                    n_copy(mb, hf, lane, dst).start()

    def lab_row_of(r):
        parts = [lab_ref[pl.ds(r * HEAD_MBS + i, 1), :] for i in range(HEAD_MBS)]
        return jnp.concatenate(parts, axis=1) - row_start

    def st_copy(r, off):
        dst = lax.rem(s + off, n_stage)
        return remote(stats.at[r, s], stats.at[r, s], st_send.at[r, off], st_recv.at[r, off], dst)

    def head_a(r):
        n_t[...] = n_all[pl.ds(r * HEAD_MBS, HEAD_MBS)].reshape(tokens, dim).T
        lab_row = lab_row_of(r)
        top, tot, lab = head_logits(n_t, emb, logits, lab_row, tokens)
        stats[r, s] = jnp.concatenate([top, tot, lab, jnp.zeros((5, tokens), F32)], axis=0)
        for off in range(1, n_stage):
            st_copy(r, off).start()

    def d_copy(r, idx):
        slot = lax.rem(idx, 2)
        dst = dt_out.at[pl.ds(pl.multiple_of(idx * tile, 16), tile), pl.ds(pl.multiple_of(r * tokens, tokens), tokens)]
        return pltpu.make_async_copy(d_stg.at[slot], dst, d_sem.at[slot])

    def head_b(r):
        for off in range(1, n_stage):
            src = lax.rem(s + n_stage - off, n_stage)
            remote(stats.at[r, s], stats.at[r, src], st_send.at[r, off], st_recv.at[r, off], src).wait_recv()
        blocks = [stats[r, i] for i in range(n_stage)]
        top = blocks[0][0:1]
        for blk in blocks[1:]:
            top = jnp.maximum(top, blk[0:1])
        tot = jnp.zeros_like(top)
        lab = jnp.zeros_like(top)
        for blk in blocks:
            tot = tot + blk[1:2] * jnp.exp2((blk[0:1] - top) * c2)
            lab = lab + blk[2:3]
        loss_acc[...] = loss_acc[...] + (jnp.log(tot) + (top - lab) * scale)
        shift = jnp.log(tot) * LOG2E - math.log2(scale)
        lab_row = lab_row_of(r)

        def tile_step(idx, _):
            @pl.when(idx >= 2)
            def _():
                d_copy(r, idx - 2).wait()
            part = head_grad_tile(idx, tile, emb, logits, d_stg.at[lax.rem(idx, 2)], lab_row, top, shift, tokens)
            gn_acc[...] = gn_acc[...] + part
            d_copy(r, idx).start()
            return 0

        gn_acc[...] = jnp.zeros_like(gn_acc)
        lax.fori_loop(0, rows // tile, tile_step, 0)
        comb[pl.ds(r * HEAD_MBS, HEAD_MBS)] = gn_acc[...].reshape(HEAD_MBS, mtok, dim).astype(BF16)
        for idx in range(rows // tile - 2, rows // tile):
            d_copy(r, idx).wait()
        for child in (0, 2, 4):
            @pl.when(s == child)
            def _(child=child):
                g_copy(r, child).start()
        for child in (1, 3):
            @pl.when(s == child)
            def _(child=child):
                g_add(r, [(buf_a, g_a)])
                g_copy(r, child).start()

    def g_copy(r, child):
        parent, slot, sem = {0: (1, buf_a, g_a), 2: (3, buf_a, g_a), 4: (5, buf_a, g_a), 1: (6, buf_a, g_a),
                             6: (7, buf_a, g_a), 3: (5, buf_b, g_b), 5: (7, buf_b, g_b)}[child]
        at = pl.ds(r * HEAD_MBS, HEAD_MBS)
        return remote(comb.at[at], slot.at[at], g_send.at[r], sem.at[r], parent)

    def g_total(r, slots):
        at = pl.ds(r * HEAD_MBS, HEAD_MBS)
        total = comb[at].astype(F32)
        for slot, sem in slots:
            remote(comb.at[at], slot.at[at], g_send.at[r], sem.at[r], 0).wait_recv()
            total = total + slot[at].astype(F32)
        return total

    def g_add(r, slots):
        comb[pl.ds(r * HEAD_MBS, HEAD_MBS)] = g_total(r, slots).astype(BF16)

    def g_mid(r):
        @pl.when(s == 6)
        def _():
            g_add(r, [(buf_a, g_a)])
            g_copy(r, 6).start()

        @pl.when(s == 5)
        def _():
            g_add(r, [(buf_a, g_a), (buf_b, g_b)])
            g_copy(r, 5).start()

    def g_final(r):
        @pl.when(s == last)
        def _():
            at = pl.ds(r * HEAD_MBS, HEAD_MBS)
            grad_n = g_total(r, [(buf_a, g_a), (buf_b, g_b)])
            x_f = x_out[at].astype(F32)
            inv = norm_scale(x_f)
            n_f = x_f * inv
            dx = inv * (grad_n - n_f * jnp.mean(grad_n * n_f, axis=-1, keepdims=True))
            comb[at] = dx.astype(BF16)
            pltpu.make_async_copy(comb.at[at], dxl_out.at[at], out_sem.at[2]).start()
            pltpu.make_async_copy(comb.at[at], dxl_out.at[at], out_sem.at[2]).wait()

    loss_acc[...] = jnp.zeros_like(loss_acc)
    first_a = HEAD_MBS + 1 + last
    n_steps = HEAD_MBS * (rounds - 1) + first_a + 4

    def step(k, _):
        for node, lead in ((3, 1), (1, 0)):
            c_mb = k + lead
            @pl.when((s == node) & (c_mb < mbs))
            def _(node=node, c_mb=c_mb):
                def comb_fwd(mb, hf):
                    add_in(mb, hf, [(buf_a, lk_a), (buf_b, lk_b)] if node == 3 else [(buf_a, lk_a)])
                    lk_copy(mb, hf, node).start()
                if node == 3:
                    @pl.when(k == 0)
                    def _():
                        halves(0, comb_fwd)
                halves(c_mb, comb_fwd)

        n_mb = k - n_stage
        @pl.when((n_mb >= 0) & (n_mb < mbs))
        def _():
            halves(n_mb, n_forward)

        f_mb = k - s
        @pl.when((f_mb >= 0) & (f_mb < mbs))
        def _():
            halves(f_mb, fwd_chunk)

        @pl.when(k == first_a)
        def _():
            @pl.when(s > 0)
            def _():
                chunks(lambda mb, hf: lk_copy(mb, hf, 1).wait_send())

        rel = k - first_a
        r = rel // HEAD_MBS
        even = lax.rem(rel + HEAD_MBS * n_stage, HEAD_MBS) == 0

        @pl.when(even & (rel >= 0) & (r < rounds))
        def _():
            head_a(r)

        @pl.when(even & (rel >= HEAD_MBS) & (r - 1 < rounds))
        def _():
            g_mid(r - 1)

        @pl.when(jnp.logical_not(even) & (rel >= 0) & (r < rounds))
        def _():
            head_b(r)

        @pl.when(jnp.logical_not(even) & (rel >= HEAD_MBS) & (r - 1 < rounds))
        def _():
            g_final(r - 1)
        return 0

    lax.fori_loop(0, n_steps, step, 0)

    out_copies = [pltpu.make_async_copy(x_in, xin_out, out_sem.at[0]), pltpu.make_async_copy(n_all, n_out, out_sem.at[1])]
    for cp in out_copies:
        cp.start()
    loss_out[...] = jnp.broadcast_to(jnp.sum(loss_acc[...], axis=1, keepdims=True), loss_out.shape)
    for c in (mbs * n_half - 2, mbs * n_half - 1):
        pre_copy(c).wait()
    for cp in out_copies:
        cp.wait()

    @pl.when(s < last)
    def _():
        chunks(lambda mb, hf: x_copy(mb, hf, 0).wait_send())
        def g_drain(r, _):
            g_copy(r, 1).wait_send()
            return 0
        lax.fori_loop(0, rounds, g_drain, 0)

    for src, count in ((last, 3), (5, 2), (3, 1), (1, 1)):
        @pl.when(s == src)
        def _(count=count):
            def drain(mb, hf):
                for lane in range(count):
                    n_copy(mb, hf, lane, 0).wait_send()
            chunks(drain)

    def st_drain(r, _):
        for off in range(1, n_stage):
            st_copy(r, off).wait_send()
        return 0
    lax.fori_loop(0, rounds, st_drain, 0)


def forward_head(n_stage, labels, part, emb, w1, w2):
    mbs, mtok, dim = part.shape
    rows = emb.shape[0]
    ffn = w1.shape[1]
    n_half = mtok // CHUNK
    chunks = mbs * n_half
    rounds = mbs // HEAD_MBS
    tokens = HEAD_MBS * mtok
    tile = vocab_tile(rows)
    any_spec = pl.BlockSpec(memory_space=pl.ANY)
    vmem_spec = pl.BlockSpec(memory_space=pltpu.VMEM)
    act = pltpu.VMEM((mbs, mtok, dim), BF16)
    dma = pltpu.SemaphoreType.DMA
    return pl.pallas_call(
        functools.partial(forward_head_kernel, n_stage),
        out_shape=(
            jax.ShapeDtypeStruct((chunks, CHUNK, ffn), F32),
            jax.ShapeDtypeStruct((mbs, mtok, dim), BF16),
            jax.ShapeDtypeStruct((mbs, mtok, dim), BF16),
            jax.ShapeDtypeStruct((rows, mbs * mtok), BF16),
            jax.ShapeDtypeStruct((mbs, mtok, dim), BF16),
            jax.ShapeDtypeStruct((8, 128), F32),
        ),
        in_specs=[vmem_spec] + [any_spec] * 4,
        out_specs=(any_spec,) * 5 + (vmem_spec,),
        scratch_shapes=[
            pltpu.VMEM((rows, dim), BF16), pltpu.VMEM((dim, ffn), BF16), pltpu.VMEM((ffn, dim), BF16),
            act, act, act, act, act, act,
            pltpu.VMEM((rows, tokens), F32), pltpu.VMEM((dim, tokens), BF16),
            pltpu.VMEM((2, CHUNK, ffn), F32), pltpu.VMEM((CHUNK, ffn), BF16),
            pltpu.VMEM((2, tile, tokens), BF16), pltpu.VMEM((tokens, dim), F32),
            pltpu.VMEM((rounds, n_stage, 8, tokens), F32), pltpu.VMEM((1, tokens), F32),
            dma((3,)), dma((mbs,)), dma((chunks,)), dma((chunks,)), dma((chunks,)),
            dma((chunks,)), dma((chunks,)), dma((3, chunks)), dma((chunks,)),
            dma((rounds, n_stage)), dma((rounds, n_stage)), dma((rounds,)), dma((rounds,)), dma((rounds,)),
            dma((2,)), dma((2,)), dma((3,)),
        ],
        compiler_params=pltpu.CompilerParams(collective_id=0, has_side_effects=True, vmem_limit_bytes=VMEM_LIMIT),
        name="forward_head",
    )(labels, part, emb, w1, w2)


def backward_kernel(
    n_stage, w1_hbm, w2_hbm, pre_hbm, dxl_hbm,
    h_out, dp_out, g_out, gx_out,
    w1, w2, g_in, g_send_buf, gx, pre_stg, h_stg, dp_stg,
    load_sem, dxl_sem, pre_sem, h_sem, dp_sem, out_sem, b_send, b_recv, x_send, x_recv,
):
    s = lax.axis_index("stage")
    last = n_stage - 1
    mbs, mtok, dim = g_in.shape
    ffn = w1.shape[1]
    width = ffn // 4

    loads = [pltpu.make_async_copy(src, dst, load_sem.at[i]) for i, (src, dst) in enumerate([(w2_hbm, w2), (w1_hbm, w1)])]
    for ld in loads:
        ld.start()

    def pre_copy(mb):
        slot = lax.rem(mb, 2)
        return pltpu.make_async_copy(pre_hbm.at[mb], pre_stg.at[slot], pre_sem.at[slot])

    pre_copy(0).start()
    pre_copy(1).start()

    @pl.when(s == last)
    def _():
        pltpu.make_async_copy(dxl_hbm, g_in, dxl_sem.at[0]).start()

    group_barrier(s, n_stage)

    @pl.when(s == last)
    def _():
        pltpu.make_async_copy(dxl_hbm, g_in, dxl_sem.at[0]).wait()
    for ld in loads:
        ld.wait()

    def b_copy(mb, dst):
        return remote(g_send_buf.at[mb], g_in.at[mb], b_send.at[mb], b_recv.at[mb], dst)

    def gx_copy(mb, lane, dst):
        return remote(gx.at[mb], gx.at[mb], x_send.at[lane, mb], x_recv.at[mb], dst)

    def hid_copies(mb):
        slot = lax.rem(mb, 2)
        return (pltpu.make_async_copy(h_stg.at[slot], h_out.at[mb], h_sem.at[slot]),
                pltpu.make_async_copy(dp_stg.at[slot], dp_out.at[mb], dp_sem.at[slot]))

    def backward_mb(mb):
        slot = lax.rem(mb, 2)

        @pl.when(s < last)
        def _():
            b_copy(mb, 0).wait_recv()

        @pl.when(mb >= 2)
        def _():
            for cp in hid_copies(mb - 2):
                cp.wait()
        pre_copy(mb).wait()
        grad = g_in[mb]
        for part in range(4):
            cols = pl.ds(part * width, width)
            dh = dot_nt(grad, w2[cols, :])
            pre = pre_stg[slot, :, cols]
            sq = pre * pre
            th = jnp.tanh(GELU_A * (pre + GELU_B * (sq * pre)))
            half_sum = 0.5 * (1.0 + th)
            h_stg[slot, :, cols] = (pre * half_sum).astype(BF16)
            slope = half_sum + (0.5 * pre) * (1.0 - th * th) * (GELU_A + (3.0 * GELU_A * GELU_B) * sq)
            dp_stg[slot, :, cols] = (dh * slope).astype(BF16)
        dx = (grad.astype(F32) + dot_nt(dp_stg[slot], w1[...])).astype(BF16)

        @pl.when(s > 0)
        def _():
            g_send_buf[mb] = dx
            b_copy(mb, s - 1).start()

        @pl.when(s == 0)
        def _():
            gx[mb] = dx
            for lane, dst in enumerate((3, last, 1)):
                gx_copy(mb, lane, dst).start()
        for cp in hid_copies(mb):
            cp.start()

        @pl.when(mb + 2 < mbs)
        def _():
            pre_copy(mb + 2).start()

    def gx_forward(mb):
        @pl.when(s > 0)
        def _():
            gx_copy(mb, 0, 0).wait_recv()
        for src, dsts in ((3, (5, 2)), (last, (6,)), (5, (4,))):
            @pl.when(s == src)
            def _(dsts=dsts):
                for lane, dst in enumerate(dsts):
                    gx_copy(mb, lane, dst).start()

    def step(k, _):
        b_mb = k - (last - s)
        @pl.when((b_mb >= 0) & (b_mb < mbs))
        def _():
            backward_mb(b_mb)

        x_mb = k - n_stage
        @pl.when((x_mb >= 0) & (x_mb < mbs))
        def _():
            gx_forward(x_mb)
        return 0

    lax.fori_loop(0, mbs + n_stage, step, 0)

    outs = [pltpu.make_async_copy(g_in, g_out, out_sem.at[0]), pltpu.make_async_copy(gx, gx_out, out_sem.at[1])]
    for cp in outs:
        cp.start()
    for mb in (mbs - 2, mbs - 1):
        for cp in hid_copies(mb):
            cp.wait()
    for cp in outs:
        cp.wait()

    @pl.when(s > 0)
    def _():
        def drain(mb, _):
            b_copy(mb, 0).wait_send()
            return 0
        lax.fori_loop(0, mbs, drain, 0)

    for src, count in ((0, 3), (3, 2), (last, 1), (5, 1)):
        @pl.when(s == src)
        def _(count=count):
            def drain(mb, _):
                for lane in range(count):
                    gx_copy(mb, lane, 0 if src != 0 else 1).wait_send()
                return 0
            lax.fori_loop(0, mbs, drain, 0)


def backward(n_stage, w1, w2, pre, dxl):
    mbs, mtok, dim = dxl.shape
    ffn = w1.shape[1]
    any_spec = pl.BlockSpec(memory_space=pl.ANY)
    act = pltpu.VMEM((mbs, mtok, dim), BF16)
    dma = pltpu.SemaphoreType.DMA
    return pl.pallas_call(
        functools.partial(backward_kernel, n_stage),
        out_shape=(
            jax.ShapeDtypeStruct((mbs, mtok, ffn), BF16),
            jax.ShapeDtypeStruct((mbs, mtok, ffn), BF16),
            jax.ShapeDtypeStruct((mbs, mtok, dim), BF16),
            jax.ShapeDtypeStruct((mbs, mtok, dim), BF16),
        ),
        in_specs=[any_spec] * 4,
        out_specs=(any_spec,) * 4,
        scratch_shapes=[
            pltpu.VMEM((dim, ffn), BF16), pltpu.VMEM((ffn, dim), BF16),
            act, act, act,
            pltpu.VMEM((2, mtok, ffn), F32), pltpu.VMEM((2, mtok, ffn), BF16), pltpu.VMEM((2, mtok, ffn), BF16),
            dma((2,)), dma((1,)), dma((2,)), dma((2,)), dma((2,)), dma((2,)),
            dma((mbs,)), dma((mbs,)), dma((3, mbs)), dma((mbs,)),
        ],
        compiler_params=pltpu.CompilerParams(collective_id=1, has_side_effects=True, vmem_limit_bytes=VMEM_LIMIT),
        name="backward",
    )(w1, w2, pre, dxl)


ROWS_E = 512
PACK = 256


def emb_grad_kernel(rows, n_stage, tok_ref, dt_ref, n_ref, gx_ref, out_ref, packed, packed_id, count_ref):
    i = pl.program_id(0)
    mbs, mtok = tok_ref.shape
    n_pack = mbs * mtok // PACK

    @pl.when(i == 0)
    def _():
        s = lax.axis_index("stage")
        loc = tok_ref[...] - s * rows
        here = (loc >= 0) & (loc < rows)
        flag = here.astype(F32)
        upper = (lax.broadcasted_iota(jnp.int32, (mtok, mtok), 0) <= lax.broadcasted_iota(jnp.int32, (mtok, mtok), 1))
        within = dot_nn(flag.astype(BF16), upper.astype(BF16))
        total = jnp.sum(flag, axis=1, keepdims=True)
        lower = (lax.broadcasted_iota(jnp.int32, (mbs, mbs), 1) < lax.broadcasted_iota(jnp.int32, (mbs, mbs), 0))
        before = jnp.sum(jnp.where(lower, jnp.transpose(jnp.broadcast_to(total, (mbs, mbs))), 0.0), axis=1, keepdims=True)
        pos = jnp.where(here, within - 1.0 + before, -1.0).astype(jnp.int32)
        count = jnp.sum(flag).astype(jnp.int32)
        count_ref[0] = count

        for b in range(n_pack):
            @pl.when(b * PACK < count)
            def _(b=b):
                slot = lax.broadcasted_iota(jnp.int32, (PACK, mtok), 0) + b * PACK
                acc = jnp.zeros((PACK, gx_ref.shape[2]), F32)
                ids = jnp.zeros((PACK, 1), F32)
                for mb in range(mbs):
                    pick = slot == pos[mb:mb + 1, :]
                    acc = acc + dot_nn(pick.astype(BF16), gx_ref[mb])
                    ids = ids + jnp.sum(jnp.where(pick, loc[mb:mb + 1, :].astype(F32), 0.0), axis=1, keepdims=True)
                filled = lax.broadcasted_iota(jnp.int32, (PACK, 1), 0) + b * PACK < count
                packed[b] = acc.astype(BF16)
                packed_id[b] = jnp.broadcast_to(jnp.where(filled, ids.astype(jnp.int32), -1), (PACK, 128))

    out_ref[...] = dot_nn(dt_ref[...], n_ref[...].reshape(mbs * mtok, n_ref.shape[2]))
    lane = lax.broadcasted_iota(jnp.int32, (PACK, ROWS_E), 1) + i * ROWS_E

    def add_pack(b, _):
        match = lane == packed_id[b][:, 0:1]
        out_ref[...] = out_ref[...] + dot_tn(match.astype(BF16), packed[b])
        return 0

    lax.fori_loop(0, (count_ref[0] + PACK - 1) // PACK, add_pack, 0)


def emb_grad(n_stage, tok, dt, n_all, gx):
    rows, total = dt.shape
    mbs, mtok, dim = gx.shape
    whole = lambda shape: pl.BlockSpec(shape, lambda i: (0,) * len(shape))
    return pl.pallas_call(
        functools.partial(emb_grad_kernel, rows, n_stage),
        grid=(pl.cdiv(rows, ROWS_E),),
        out_shape=jax.ShapeDtypeStruct((rows, dim), F32),
        in_specs=[whole((mbs, mtok)), pl.BlockSpec((ROWS_E, total), lambda i: (i, 0)), whole((mbs, mtok, dim)), whole((mbs, mtok, dim))],
        out_specs=pl.BlockSpec((ROWS_E, dim), lambda i: (i, 0)),
        scratch_shapes=[
            pltpu.VMEM((total // PACK, PACK, dim), BF16),
            pltpu.VMEM((total // PACK, PACK, 128), jnp.int32),
            pltpu.SMEM((1,), jnp.int32),
        ],
        compiler_params=pltpu.CompilerParams(vmem_limit_bytes=50_000_000),
        name="emb_grad",
    )(tok, dt, n_all, gx)


def solution(mesh):
    n_stage = mesh.shape["stage"]

    def stage_body(token_ids, label_ids, emb_rows, w_in, w_out):
        stage_idx = lax.axis_index("stage")
        mbs, mtok = token_ids.shape
        rows, dim = emb_rows.shape
        ffn = w_in.shape[2]
        w1 = w_in[0]
        w2 = w_out[0]
        local_tok = token_ids - stage_idx * rows
        tok_here = (local_tok >= 0) & (local_tok < rows)
        looked_up = jnp.take(emb_rows, jnp.clip(local_tok, 0, rows - 1), axis=0)
        part = jnp.where(tok_here[..., None], looked_up, 0)

        pre, x_in, n_all, dt, dxl, loss = forward_head(n_stage, label_ids, part, emb_rows, w1, w2)
        hid, dpre, g_all, gx = backward(n_stage, w1, w2, pre.reshape(mbs, mtok, ffn), dxl)
        tokens = mbs * mtok
        grad_in = dot_tn(x_in.reshape(tokens, dim), dpre.reshape(tokens, ffn))
        grad_out = dot_tn(hid.reshape(tokens, ffn), g_all.reshape(tokens, dim))
        grad_emb = emb_grad(n_stage, token_ids, dt, n_all, gx)
        mean_loss = (loss[0, 0] / tokens).reshape(1)
        return mean_loss, grad_in[None], grad_out[None], grad_emb

    return jax.shard_map(
        stage_body,
        mesh=mesh,
        in_specs=(P("dp", None), P("dp", None), P("stage", None), P("stage", None, None), P("stage", None, None)),
        out_specs=(P("dp"), P(("dp", "stage"), None, None), P(("dp", "stage"), None, None), P(("dp", "stage"), None)),
        check_vma=False,
    )
```

time: 1840 us -> 431 us (0.23)
  the two profiles are of different devices: /device:TPU:122 before, /device:TPU:84 now
where the time goes in v1:
time: 431 us
  Pallas kernels  377 us (87%)
  matrix products  29.4 us (7%)
  local copies, waits for them, and re-layouts  18.4 us (4%)
    pallas_call x1, Pallas kernels, forward_head(): pl.pallas_call(functools.partial(forward_head_kernel, n_stage), out_shape...  187 us
    pallas_call x1, Pallas kernels, backward(): pl.pallas_call(functools.partial(backward_kernel, n_stage), out_shape=(ja...  149 us
    pallas_call x1, Pallas kernels, emb_grad(): pl.pallas_call(functools.partial(emb_grad_kernel, rows, n_stage), grid=(p...  41.5 us
    dot_general x2, matrix products, dot_tn(): lax.dot_general(a, b, (((0,), (0,)), ((), ())), preferred_element_type=F32)  29.4 us
    gather x1, local copies, waits for them, and re-layouts, stage_body(): looked_up = jnp.take(emb_rows, jnp.clip(local_tok, 0, rows - 1), axis=0)  13.4 us

profile of v1, /device:TPU:84, one launch (start us, length us, event | category | flops | bytes accessed | tf_op | source)
XLA Modules:
  0.0 430.7 jit_solution(9460499237629910408)
XLA Ops:
  0.6 0.7 compare_and_fusion.1
  1.3 0.7 fusion
  2.1 13.4 %gather_fusion = bf16[2048,768]{1,0:T(8,128)(2,1)S(1)} fusion(bf16[6288,768]{1,0:T(8,128)(2,1)} %emb_hbm.1, s32[2048]{0:T(1024)S(1)} %broadcast_clamp_fusion), kind=kCustom, calls=%fused_computation | custom fusion | bytes 6299648 | tf_op jit(solution)/shard_map/jit(_take)/gather | solution.py:744
  15.5 2.0 select_select_fusion.part_hbm
  17.6 186.8 %forward_head.1 = (f32[16,128,3072]{2,1,0:T(8,128)}, bf16[8,256,768]{2,1,0:T(8,128)(2,1)}, bf16[8,256,768]{2,1,0:T(8,128)(2,1)}, bf16[6288,2048]{1,0:T(8,128)(2,...) custom-call(s32[8,256]{1,0:T(8,128)} %lab_ref.1, bf16[8,256,768]{2,1,0:T(8,128)(2,1)} %select_select_fusion.part_hbm, ...), custom_call_target="tpu_custom_call" | custom-call | tf_op jit(solution)/shard_map/forward_head/pallas_call | solution.py:468
  204.4 1.2 slice.3
  206.2 0.0 copy-start.2
  206.2 148.7 %backward.1 = (bf16[8,256,3072]{2,1,0:T(8,128)(2,1)}, bf16[8,256,3072]{2,1,0:T(8,128)(2,1)}, bf16[8,256,768]{2,1,0:T(8,128)(2,1)}, bf16[8,256,768]{2,1,0:T(8,128)(2,1)}) custom-call(bf16[768,3072]{1,0:T(8,128)(2,1)} %bitcast.20, bf16[3072,768]{1,0:T(8,128)(2,1)} %bitcast.22, f32[8,256,3072]{2,1,0:T(8,128)} %bitcast.18, ...), custom_call_target="tpu_custom_call" | custom-call | tf_op jit(solution)/shard_map/backward/pallas_call | solution.py:641
  354.9 0.0 copy-done.2
  354.9 0.0 copy-start
  355.0 1.9 copy-done
  356.8 0.0 copy-start.1
  356.8 1.9 copy-done.1
  358.7 0.0 slice-start
  358.7 0.0 slice-start.1
  358.7 41.5 %emb_grad.1 = f32[6288,768]{1,0:T(8,128)} custom-call(s32[8,256]{1,0:T(8,128)S(1)} %copy-done.2, bf16[6288,2048]{1,0:T(8,128)(2,1)} %get-tuple-element.21.dt_ref, bf16[8,256,768]{2,1,0:T(8,128)(2,1)S(1)} %copy-done, bf16[8,256,768]{2,1,0:T(8,128)(2,1)S(1)} %copy-done.1), custom_call_target="tpu_custom_call" | custom-call | tf_op jit(solution)/shard_map/emb_grad/pallas_call | solution.py:716
  400.2 0.0 slice-start.2
  400.2 0.0 copy-start.3
  400.2 16.5 %convolution_bitcast_fusion.1 = f32[1,768,3072]{2,1,0:T(8,128)} fusion(bf16[8,256,768]{2,1,0:T(8,128)(2,1)} %get-tuple-element.15, bf16[8,256,3072]{2,1,0:T(8,128)(2,1)} %get-tuple-element.18), kind=kOutput, calls=%fused_computation.2 | convolution fusion | flops 9663676416 | bytes 25165824 | tf_op jit(solution)/shard_map/dot_general | solution.py:32
  416.7 0.0 slice-done
  416.7 0.0 slice-done.1
  416.7 0.0 slice-done.2
  416.7 0.0 copy-done.3
  416.7 12.9 %convolution_bitcast_fusion = f32[1,3072,768]{2,1,0:T(8,128)} fusion(bf16[8,256,3072]{2,1,0:T(8,128)(2,1)S(1)} %bitcast.26, bf16[8,256,768]{2,1,0:T(8,128)(2,1)S(1)} %copy-done.3), kind=kOutput, calls=%fused_computation.1 | convolution fusion | flops 9663676416 | bytes 25165824 | tf_op jit(solution)/shard_map/dot_general | solution.py:32
  (3 shorter events, 0.0 us)
Async XLA Ops:
  206.2 148.7 %copy-start.2 = (s32[8,256]{1,0:T(8,128)S(1)}, s32[8,256]{1,0:T(8,128)}, u32[]{:S(2)}) copy-start(s32[8,256]{1,0:T(8,128)} %tok_ref.1) | copy-start | bytes 24580
  354.9 1.9 copy-start
  356.8 1.9 copy-start.1
  358.7 58.0 %slice-start = ((s8[12582912]{0:T(1024)(128)(4,1)}), s8[4194304]{0:T(1024)(128)(4,1)S(1)}, s32[]{:S(2)}) async-start(s8[12582912]{0:T(1024)(128)(4,1)} %bitcast.25), calls=%async_computation | async-start | bytes 8388608
  358.7 58.0 %slice-start.1 = ((s8[12582912]{0:T(1024)(128)(4,1)}), s8[4194304]{0:T(1024)(128)(4,1)S(1)}, s32[]{:S(2)}) async-start(s8[12582912]{0:T(1024)(128)(4,1)} %bitcast.25), calls=%async_computation.1 | async-start | bytes 8388608
  400.2 16.5 %slice-start.2 = ((s8[12582912]{0:T(1024)(128)(4,1)}), s8[4194304]{0:T(1024)(128)(4,1)S(1)}, s32[]{:S(2)}) async-start(s8[12582912]{0:T(1024)(128)(4,1)} %bitcast.25), calls=%async_computation.2 | async-start | bytes 8388608
  400.2 16.5 %copy-start.3 = (bf16[8,256,768]{2,1,0:T(8,128)(2,1)S(1)}, bf16[8,256,768]{2,1,0:T(8,128)(2,1)}, u32[]{:S(2)}) copy-start(bf16[8,256,768]{2,1,0:T(8,128)(2,1)} %get-tuple-element.20) | copy-start | bytes 9437188

commit v2 on v0

v2 whole, which is shorter than its diff:
```python
import functools
import math

import jax
import jax.numpy as jnp
from jax import lax
from jax.experimental import pallas as pl
from jax.experimental.pallas import tpu as pltpu
from jax.sharding import PartitionSpec as P

NORM_EPS = 1e-6
MESH = pl.DeviceIdType.MESH
F32 = jnp.float32
BF16 = jnp.bfloat16
GELU_A = math.sqrt(2.0 / math.pi)
GELU_B = 0.044715
LOG2E = math.log2(math.e)
CHUNK = 128
HEAD_MBS = 2
VMEM_LIMIT = 67_000_000


def dot_nn(a, b):
    return lax.dot_general(a, b, (((1,), (0,)), ((), ())), preferred_element_type=F32)


def dot_nt(a, b):
    return lax.dot_general(a, b, (((1,), (1,)), ((), ())), preferred_element_type=F32)


def dot_tn(a, b):
    return lax.dot_general(a, b, (((0,), (0,)), ((), ())), preferred_element_type=F32)


def gelu_and_slope(pre):
    sq = pre * pre
    th = jnp.tanh(pre * (GELU_A + (GELU_A * GELU_B) * sq))
    half_sum = 0.5 + 0.5 * th
    hid = pre * half_sum
    slope = half_sum + (hid - hid * th) * (GELU_A + (3.0 * GELU_A * GELU_B) * sq)
    return hid, slope


def norm_scale(x_f32):
    return lax.rsqrt(jnp.mean(x_f32 * x_f32, axis=-1, keepdims=True) + NORM_EPS)


def remote(src, dst, send_sem, recv_sem, stage):
    return pltpu.make_async_remote_copy(
        src_ref=src, dst_ref=dst, send_sem=send_sem, recv_sem=recv_sem, device_id={"stage": stage}, device_id_type=MESH
    )


def group_barrier(stage, n_stage):
    barrier = pltpu.get_barrier_semaphore()
    for off in range(1, n_stage):
        pl.semaphore_signal(barrier, inc=1, device_id={"stage": lax.rem(stage + off, n_stage)}, device_id_type=MESH)
    pl.semaphore_wait(barrier, n_stage - 1)


def vocab_tile(rows):
    for parts in range(2, rows + 1):
        if rows % parts == 0 and (rows // parts) % 16 == 0 and rows // parts <= 2400:
            return rows // parts
    return rows


def sub_blocks(rows, size):
    return [(start, min(size, rows - start)) for start in range(0, rows, size)]


def forward_chunk(x, w1, w2, slope_slot, hid_slot):
    ffn = w1.shape[1]
    width = ffn // 4
    for part in range(4):
        cols = pl.ds(part * width, width)
        hid, slope = gelu_and_slope(dot_nn(x, w1[:, cols]))
        slope_slot[:, cols] = slope
        hid_slot[:, cols] = hid.astype(BF16)
    return x.astype(F32) + dot_nn(hid_slot[...], w2[...])


def backward_chunk(grad, wt, slope_slot, dpre_slot):
    ffn = slope_slot.shape[1]
    dim = grad.shape[1]
    for part in range(ffn // dim):
        cols = pl.ds(part * dim, dim)
        d_hid = dot_nn(grad, wt[pl.ds(ffn + part * dim, dim), :])
        dpre_slot[:, cols] = (d_hid * slope_slot[:, cols]).astype(BF16)
    return grad.astype(F32) + dot_nn(dpre_slot[...], wt[pl.ds(0, ffn), :])


def transpose_weights(w1, w2, wt):
    dim, ffn = w1.shape
    for part in range(ffn // dim):
        at = pl.ds(part * dim, dim)
        wt[at, :] = w1[:, at].T
        wt[pl.ds(ffn + part * dim, dim), :] = w2[at, :].T


def head_logits(n_t, emb, logits, lab_row, tokens):
    rows = emb.shape[0]
    tile = vocab_tile(rows)
    c2 = LOG2E * emb.shape[1] ** -0.5

    def tile_step(idx, carry):
        mx, sm, lb = carry
        base = pl.multiple_of(idx * tile, 16)
        for start, size in sub_blocks(tile, 256):
            at = pl.ds(base + start, size)
            block = dot_nn(emb[at, :], n_t[...])
            logits[at, :] = block
            b3 = block.reshape(size // 8, 8, tokens)
            row_ids = lax.broadcasted_iota(jnp.int32, (size, tokens), 0) + (base + start)
            hit = jnp.where(row_ids == lab_row, block, 0.0).reshape(size // 8, 8, tokens)
            mx_new = jnp.maximum(mx, jnp.max(b3, axis=0))
            sm = sm * jnp.exp2((mx - mx_new) * c2) + jnp.sum(jnp.exp2((b3 - mx_new[None]) * c2), axis=0)
            lb = lb + jnp.sum(hit, axis=0)
            mx = mx_new
        return mx, sm, lb

    init = (jnp.full((8, tokens), -3.0e38, F32), jnp.zeros((8, tokens), F32), jnp.zeros((8, tokens), F32))
    mx, sm, lb = lax.fori_loop(0, rows // tile, tile_step, init)
    top = jnp.max(mx, axis=0, keepdims=True)
    tot = jnp.sum(sm * jnp.exp2((mx - top) * c2), axis=0, keepdims=True)
    lab = jnp.sum(lb, axis=0, keepdims=True)
    return top, tot, lab


def head_grad_tile(base, size_all, emb, logits, d_slot, lab_row, top, shift, tokens):
    scale = emb.shape[1] ** -0.5
    c2 = LOG2E * scale
    total = None
    for start, size in sub_blocks(size_all, 256):
        at = pl.ds(base + start, size)
        row_ids = lax.broadcasted_iota(jnp.int32, (size, tokens), 0) + (base + start)
        prob = jnp.exp2((logits[at, :] - top) * c2 - shift)
        d_log = (prob - jnp.where(row_ids == lab_row, scale, 0.0)).astype(BF16)
        d_slot[pl.ds(start, size), :] = d_log
        part = dot_tn(d_log, emb[at, :])
        total = part if total is None else total + part
    return total


E_ROWS = 512
LOOKUP_LEAD = 1
LOOKUP_PARENT = {2: (3, 0), 1: (0, 0), 4: (5, 0), 6: (7, 0), 5: (3, 1), 7: (0, 1), 3: (0, 2)}
GRAD_PARENT = {0: (1, 0), 2: (3, 0), 4: (5, 0), 1: (6, 0), 6: (7, 0), 3: (5, 1), 5: (7, 1)}


def step_kernel(
    n_stage, lab_ref, part_hbm, emb_hbm, w1_hbm, w2_hbm,
    slope_out, hid_out, dpre_out, xin_out, n_out, g_out, gx_out, dt_out, ge_out, loss_out,
    emb, w1, w2, x_in, x_out, n_all, comb, buf_a, buf_b, slope_stg, act_stg, stats, loss_acc,
    load_sem, part_sem, lk_send, lk_a, lk_b, lk_c, x_send, x_recv, n_send, n_recv, st_send, st_recv,
    g_send, g_a, g_b, b_send, b_recv, gx_send, gx_recv, slope_sem, act_sem, d_sem, e_sem, out_sem, gx_sem,
):
    s = lax.axis_index("stage")
    last = n_stage - 1
    mbs, mtok, dim = x_in.shape
    n_half = mtok // CHUNK
    n_chunks = mbs * n_half
    rows = emb.shape[0]
    ffn = w1.shape[1]
    tile = vocab_tile(rows)
    tokens = HEAD_MBS * mtok
    rounds = mbs // HEAD_MBS
    scale = dim ** -0.5
    c2 = LOG2E * scale
    row_start = s * rows
    bufs = (buf_a, buf_b, x_in)
    lk_sems = (lk_a, lk_b, lk_c)

    loads = [pltpu.make_async_copy(src, dst, load_sem.at[i])
             for i, (src, dst) in enumerate([(w1_hbm, w1), (w2_hbm, w2), (emb_hbm, emb)])]
    for mb in range(mbs):
        pltpu.make_async_copy(part_hbm.at[mb], comb.at[mb], part_sem.at[mb]).start()
    for ld in loads:
        ld.start()
    group_barrier(s, n_stage)

    def pos(c):
        return (c // n_half, pl.ds(pl.multiple_of(lax.rem(c, n_half) * CHUNK, CHUNK), CHUNK))

    def at_chunk(ref, c):
        return ref.at[c // n_half, pl.ds(pl.multiple_of(lax.rem(c, n_half) * CHUNK, CHUNK), CHUNK)]

    def loop(lo, hi, fn):
        def body(i, _):
            fn(i)
            return 0
        lax.fori_loop(lo, hi, body, 0)

    def chunks_of(mb, fn):
        loop(mb * n_half, (mb + 1) * n_half, fn)

    def each_role(roles, fn):
        for node in roles:
            @pl.when(s == node)
            def _(node=node):
                fn(node)

    def lk_copy(c, child):
        parent, slot = LOOKUP_PARENT[child]
        return remote(at_chunk(comb, c), at_chunk(bufs[slot], c), lk_send.at[c], lk_sems[slot].at[c], parent)

    def lk_total(c, slots):
        total = comb[pos(c)].astype(F32)
        for slot in range(slots):
            remote(at_chunk(comb, c), at_chunk(bufs[slot], c), lk_send.at[c], lk_sems[slot].at[c], 0).wait_recv()
            total = total + bufs[slot][pos(c)].astype(F32)
        return total.astype(BF16)

    def lk_forward(c, node, slots):
        comb[pos(c)] = lk_total(c, slots)
        lk_copy(c, node).start()

    loop(0, mbs, lambda mb: pltpu.make_async_copy(part_hbm.at[mb], comb.at[mb], part_sem.at[mb]).wait())
    each_role((1, 2, 4, 6), lambda node: loop(0, n_chunks, lambda c: lk_copy(c, node).start()))
    each_role((5, 7), lambda node: loop(0, n_chunks, lambda c: lk_forward(c, node, 1)))
    loads[0].wait()
    loads[1].wait()

    n_routes = {last: (5, 1, 6), 5: (4,), 1: (3, 0), 3: (2,)}

    def x_copy(c, dst_stage):
        return remote(at_chunk(x_out, c), at_chunk(x_in, c), x_send.at[c], x_recv.at[c], dst_stage)

    def n_copy(c, lane, dst_stage):
        return remote(at_chunk(n_all, c), at_chunk(n_all, c), n_send.at[lane, c], n_recv.at[c], dst_stage)

    def fwd_copies(c):
        slot = lax.rem(c, 2)
        return (pltpu.make_async_copy(slope_stg.at[slot], slope_out.at[c], slope_sem.at[slot]),
                pltpu.make_async_copy(act_stg.at[slot], hid_out.at[c], act_sem.at[slot]))

    def fwd_chunk(c):
        idx = pos(c)

        @pl.when(s == 0)
        def _():
            x_in[idx] = lk_total(c, 3)

        @pl.when(s > 0)
        def _():
            x_copy(c, 0).wait_recv()

        @pl.when(c >= 2)
        def _():
            for cp in fwd_copies(c - 2):
                cp.wait()

        slot = lax.rem(c, 2)
        out = forward_chunk(x_in[idx], w1, w2, slope_stg.at[slot], act_stg.at[slot]).astype(BF16)
        x_out[idx] = out
        for cp in fwd_copies(c):
            cp.start()

        @pl.when(s < last)
        def _():
            x_copy(c, s + 1).start()

        @pl.when(s == last)
        def _():
            out_f = out.astype(F32)
            n_all[idx] = (out_f * norm_scale(out_f)).astype(BF16)
            for lane, dst in enumerate(n_routes[last]):
                n_copy(c, lane, dst).start()

    def n_round(r, fn):
        loop(r * HEAD_MBS * n_half, (r + 1) * HEAD_MBS * n_half, fn)

    def n_early(r):
        def take(c, node):
            n_copy(c, 0, 0 if node == last else last).wait_recv()
            for lane, dst in enumerate(n_routes[node]):
                n_copy(c, lane, dst).start()
        each_role((1, 5), lambda node: n_round(r, lambda c: take(c, node)))

    def n_mid(r):
        def take(c, node):
            n_copy(c, 0, last).wait_recv()
            n_copy(c, 0, n_routes[node][0]).start()
        each_role((3,), lambda node: n_round(r, lambda c: take(c, node)))

    def n_late(r):
        @pl.when((lax.rem(s, 2) == 0))
        def _():
            n_round(r, lambda c: n_copy(c, 0, last).wait_recv())

    def g_copy(mb, child):
        parent, slot = GRAD_PARENT[child]
        return remote(comb.at[mb], bufs[slot].at[mb], g_send.at[mb], (g_a, g_b)[slot].at[mb], parent)

    def g_total(mb, slots):
        total = comb[mb].astype(F32)
        for slot in range(slots):
            remote(comb.at[mb], bufs[slot].at[mb], g_send.at[mb], (g_a, g_b)[slot].at[mb], 0).wait_recv()
            total = total + bufs[slot][mb].astype(F32)
        return total

    def g_forward(mb, node, slots):
        comb[mb] = g_total(mb, slots).astype(BF16)
        g_copy(mb, node).start()

    def g_low(r):
        each_role((1, 3), lambda node: loop(r * HEAD_MBS, (r + 1) * HEAD_MBS, lambda mb: g_forward(mb, node, 1)))

    def g_mid(r):
        each_role((6,), lambda node: loop(r * HEAD_MBS, (r + 1) * HEAD_MBS, lambda mb: g_forward(mb, node, 1)))
        each_role((5,), lambda node: loop(r * HEAD_MBS, (r + 1) * HEAD_MBS, lambda mb: g_forward(mb, node, 2)))

    def g_final(mb):
        @pl.when(s == last)
        def _():
            grad_n = g_total(mb, 2)
            x_f = x_out[mb].astype(F32)
            inv = norm_scale(x_f)
            n_f = x_f * inv
            dx = inv * (grad_n - n_f * jnp.mean(grad_n * n_f, axis=-1, keepdims=True))
            comb[mb] = dx.astype(BF16)

    def lab_row_of(r):
        parts = [lab_ref[pl.ds(r * HEAD_MBS + i, 1), :] for i in range(HEAD_MBS)]
        return jnp.concatenate(parts, axis=1) - row_start

    def st_copy(r, off):
        dst = lax.rem(s + off, n_stage)
        return remote(stats.at[r, s], stats.at[r, s], st_send.at[r, off], st_recv.at[r, off], dst)

    saves = [pltpu.make_async_copy(x_in, xin_out, out_sem.at[0]), pltpu.make_async_copy(n_all, n_out, out_sem.at[1])]

    def forward_and_head(logits, n_t, d_stg, gn_acc):
        n_tiles = rows // tile

        def head_a(r):
            n_late(r)

            @pl.when(r == rounds - 1)
            def _():
                for cp in saves:
                    cp.start()

            n_t[...] = n_all[pl.ds(r * HEAD_MBS, HEAD_MBS)].reshape(tokens, dim).T
            top, tot, lab = head_logits(n_t, emb, logits, lab_row_of(r), tokens)

            @pl.when(r == rounds - 1)
            def _():
                for cp in saves:
                    cp.wait()

                @pl.when(s < last)
                def _():
                    loop(0, n_chunks, lambda c: x_copy(c, 0).wait_send())
                for src, dsts in n_routes.items():
                    @pl.when(s == src)
                    def _(dsts=dsts):
                        loop(0, n_chunks, lambda c: [n_copy(c, lane, dst).wait_send() for lane, dst in enumerate(dsts)])
            stats[r, s] = jnp.concatenate([top, tot, lab, jnp.zeros((5, tokens), F32)], axis=0)
            for off in range(1, n_stage):
                st_copy(r, off).start()

        def d_copy(seq):
            slot = lax.rem(seq, 2)
            r = seq // n_tiles
            idx = lax.rem(seq, n_tiles)
            dst = dt_out.at[pl.ds(pl.multiple_of(idx * tile, 16), tile), pl.ds(pl.multiple_of(r * tokens, tokens), tokens)]
            return pltpu.make_async_copy(d_stg.at[slot], dst, d_sem.at[slot])

        def head_b(r):
            @pl.when(r + 1 < rounds)
            def _():
                n_early(r + 1)
            for off in range(1, n_stage):
                src = lax.rem(s + n_stage - off, n_stage)
                remote(stats.at[r, s], stats.at[r, src], st_send.at[r, off], st_recv.at[r, off], src).wait_recv()
            blocks = [stats[r, i] for i in range(n_stage)]
            top = blocks[0][0:1]
            for blk in blocks[1:]:
                top = jnp.maximum(top, blk[0:1])
            tot = jnp.zeros_like(top)
            lab = jnp.zeros_like(top)
            for blk in blocks:
                tot = tot + blk[1:2] * jnp.exp2((blk[0:1] - top) * c2)
                lab = lab + blk[2:3]
            loss_acc[...] = loss_acc[...] + (jnp.log(tot) + (top - lab) * scale)
            shift = jnp.log(tot) * LOG2E - math.log2(scale)
            lab_row = lab_row_of(r)

            def tile_step(idx):
                seq = r * n_tiles + idx

                @pl.when(seq >= 2)
                def _():
                    d_copy(seq - 2).wait()
                @pl.when((idx == n_tiles - 1) & (r + 1 < rounds))
                def _():
                    n_mid(r + 1)
                base = pl.multiple_of(idx * tile, 16)
                part = head_grad_tile(base, tile, emb, logits, d_stg.at[lax.rem(seq, 2)], lab_row, top, shift, tokens)
                gn_acc[...] = gn_acc[...] + part
                d_copy(seq).start()

            gn_acc[...] = jnp.zeros_like(gn_acc)
            loop(0, n_tiles, tile_step)
            comb[pl.ds(r * HEAD_MBS, HEAD_MBS)] = gn_acc[...].reshape(HEAD_MBS, mtok, dim).astype(BF16)
            each_role((0, 2, 4), lambda node: loop(r * HEAD_MBS, (r + 1) * HEAD_MBS, lambda mb: g_copy(mb, node).start()))
        loss_acc[...] = jnp.zeros_like(loss_acc)
        first_a = HEAD_MBS + 1 + last

        def step(k):
            @pl.when((s == 3) & (k == 0))
            def _():
                loop(0, LOOKUP_LEAD * n_half, lambda c: lk_forward(c, 3, 2))

            @pl.when((s == 3) & (k + LOOKUP_LEAD < mbs))
            def _():
                chunks_of(k + LOOKUP_LEAD, lambda c: lk_forward(c, 3, 2))

            f_mb = k - s

            @pl.when((f_mb >= 0) & (f_mb < mbs))
            def _():
                chunks_of(f_mb, fwd_chunk)

            @pl.when(k == first_a)
            def _():
                loads[2].wait()

                @pl.when(s > 0)
                def _():
                    loop(0, n_chunks, lambda c: lk_copy(c, 1).wait_send())

            rel = k - first_a
            r = rel // HEAD_MBS
            even = lax.rem(rel + HEAD_MBS * n_stage, HEAD_MBS) == 0

            @pl.when(k == first_a)
            def _():
                n_early(0)
                n_mid(0)

            @pl.when(even & (rel >= 0))
            def _():
                head_a(r)

            @pl.when(even & (rel >= HEAD_MBS))
            def _():
                g_low(r - 1)

                @pl.when(r >= 2)
                def _():
                    loop((r - 2) * HEAD_MBS, (r - 1) * HEAD_MBS, g_final)

            @pl.when(jnp.logical_not(even) & (rel >= 0))
            def _():
                head_b(r)

            @pl.when(jnp.logical_not(even) & (rel >= HEAD_MBS))
            def _():
                g_mid(r - 1)

        loop(0, first_a + HEAD_MBS * rounds, step)
        for c in (n_chunks - 2, n_chunks - 1):
            for cp in fwd_copies(c):
                cp.wait()
        for seq in (rounds * n_tiles - 2, rounds * n_tiles - 1):
            d_copy(seq).wait()

    pl.run_scoped(
        forward_and_head,
        pltpu.VMEM((rows, tokens), F32), pltpu.VMEM((dim, tokens), BF16),
        pltpu.VMEM((2, tile, tokens), BF16), pltpu.VMEM((tokens, dim), F32),
    )
    loss_out[...] = jnp.broadcast_to(jnp.sum(loss_acc[...], axis=1, keepdims=True), loss_out.shape)

    g_in, g_buf, gx, wt = x_in, x_out, n_all, emb

    def b_copy(c, dst):
        return remote(at_chunk(g_buf, c), at_chunk(g_in, c), b_send.at[c], b_recv.at[c], dst)

    def gx_copy(c, lane, dst):
        return remote(at_chunk(gx, c), at_chunk(gx, c), gx_send.at[lane, c], gx_recv.at[c], dst)

    def slope_copy(c):
        slot = lax.rem(c, 2)
        return pltpu.make_async_copy(slope_out.at[c], slope_stg.at[slot], slope_sem.at[slot])

    def dpre_copy(c):
        slot = lax.rem(c, 2)
        return pltpu.make_async_copy(act_stg.at[slot], dpre_out.at[c], act_sem.at[slot])

    gx_split = n_chunks // 2
    gx_routes = {0: ((3, 0, n_chunks), (last, 0, n_chunks), (1, 0, n_chunks)), 3: ((2, 0, n_chunks), (5, 0, gx_split)),
                 last: ((6, 0, n_chunks), (5, gx_split, n_chunks)), 5: ((4, 0, n_chunks),)}

    def gx_send_all(c, node):
        for lane, (dst, lo, hi) in enumerate(gx_routes[node]):
            @pl.when((c >= lo) & (c < hi))
            def _(lane=lane, dst=dst):
                gx_copy(c, lane, dst).start()


    def bwd_chunk(c):
        slot = lax.rem(c, 2)
        idx = pos(c)

        @pl.when(s < last)
        def _():
            b_copy(c, 0).wait_recv()

        @pl.when(s == last)
        def _():
            g_in[idx] = comb[idx]

        @pl.when(c >= 2)
        def _():
            dpre_copy(c - 2).wait()
        slope_copy(c).wait()
        dx = backward_chunk(g_in[idx], wt, slope_stg.at[slot], act_stg.at[slot]).astype(BF16)

        @pl.when(s > 0)
        def _():
            g_buf[idx] = dx
            b_copy(c, s - 1).start()

        @pl.when(s == 0)
        def _():
            gx[idx] = dx
            gx_send_all(c, 0)
        dpre_copy(c).start()

        @pl.when(c + 2 < n_chunks)
        def _():
            slope_copy(c + 2).start()

    full = rows // E_ROWS
    rest = rows - full * E_ROWS

    def backward(n_rows, d_in, e_stg):
        def d_load(i, size=E_ROWS):
            slot = lax.rem(i, 2)
            src = dt_out.at[pl.ds(pl.multiple_of(i * E_ROWS, E_ROWS), size)]
            return pltpu.make_async_copy(src, d_in.at[slot, pl.ds(0, size)], d_sem.at[slot])

        def e_save(i, size=E_ROWS):
            slot = lax.rem(i, 2)
            dst = ge_out.at[pl.ds(pl.multiple_of(i * E_ROWS, E_ROWS), size)]
            return pltpu.make_async_copy(e_stg.at[slot, pl.ds(0, size)], dst, e_sem.at[slot])

        def e_tile(i):
            slot = lax.rem(i, 2)

            @pl.when(i + 1 < full)
            def _():
                d_load(i + 1).start()
            if rest:
                @pl.when(i + 1 == full)
                def _():
                    d_load(full, rest).start()
            d_load(i).wait()

            @pl.when(i >= 2)
            def _():
                e_save(i - 2).wait()
            e_stg[slot] = dot_nn(d_in[slot], n_rows[...].reshape(mbs * mtok, dim))
            e_save(i).start()

        n_load = pltpu.make_async_copy(n_out, n_rows, out_sem.at[1])
        n_load.start()
        slope_copy(0).start()
        slope_copy(1).start()
        d_load(0).start()
        g_low(rounds - 1)
        transpose_weights(w1, w2, wt)
        n_load.wait()
        early = jnp.minimum((last - s) * 2, full)
        loop(0, early, e_tile)

        def gx_save(c):
            return pltpu.make_async_copy(at_chunk(gx, c), at_chunk(gx_out, c), gx_sem.at[c])

        def gx_forward(c):
            @pl.when(s > 0)
            def _():
                gx_copy(c, 0, 0).wait_recv()
            each_role((3, last, 5), lambda node: gx_send_all(c, node))
            gx_save(c).start()

        def step(k):
            @pl.when(k >= mbs - 2 * HEAD_MBS)
            def _():
                @pl.when(k < mbs)
                def _():
                    g_final(k)
            b_mb = k - (last - s)

            @pl.when((b_mb >= 0) & (b_mb < mbs))
            def _():
                chunks_of(b_mb, bwd_chunk)

            @pl.when(k == 2)
            def _():
                g_mid(rounds - 1)

            x_mb = k - n_stage

            @pl.when((s == 3) & (x_mb >= 0) & (x_mb < gx_split // n_half))
            def _():
                chunks_of(x_mb, gx_forward)

        loop(0, mbs + last, step)
        g_save = pltpu.make_async_copy(g_in, g_out, out_sem.at[0])
        g_save.start()
        loop(early, full, e_tile)
        loop(jnp.where(s == 3, gx_split, 0), n_chunks, gx_forward)
        if rest:
            d_load(full, rest).wait()
            e_save(full - 2).wait()
            slot = full % 2
            e_stg[slot, pl.ds(0, rest)] = dot_nn(d_in[slot, pl.ds(0, rest)], n_rows[...].reshape(mbs * mtok, dim))
            e_save(full, rest).start()

        g_save.wait()
        if rest:
            e_save(full - 1).wait()
            e_save(full, rest).wait()
        else:
            e_save(full - 2).wait()
            e_save(full - 1).wait()
        for c in (n_chunks - 2, n_chunks - 1):
            dpre_copy(c).wait()
        loop(0, n_chunks, lambda c: gx_save(c).wait())

    pl.run_scoped(
        backward,
        pltpu.VMEM((mbs, mtok, dim), BF16), pltpu.VMEM((2, E_ROWS, mbs * mtok), BF16), pltpu.VMEM((2, E_ROWS, dim), F32),
    )

    @pl.when(s < last)
    def _():
        loop(0, mbs, lambda mb: g_copy(mb, 1).wait_send())

    @pl.when(s > 0)
    def _():
        loop(0, n_chunks, lambda c: b_copy(c, 0).wait_send())
    for src, routes in gx_routes.items():
        @pl.when(s == src)
        def _(routes=routes):
            for lane, (dst, lo, hi) in enumerate(routes):
                loop(lo, hi, lambda c: gx_copy(c, lane, dst).wait_send())
    loop(0, rounds, lambda r: [st_copy(r, off).wait_send() for off in range(1, n_stage)])


def pipeline_step(n_stage, labels, part, emb, w1, w2):
    mbs, mtok, dim = part.shape
    rows = emb.shape[0]
    ffn = w1.shape[1]
    chunks = mbs * mtok // CHUNK
    rounds = mbs // HEAD_MBS
    tokens = HEAD_MBS * mtok
    any_spec = pl.BlockSpec(memory_space=pl.ANY)
    vmem_spec = pl.BlockSpec(memory_space=pltpu.VMEM)
    act = pltpu.VMEM((mbs, mtok, dim), BF16)
    dma = pltpu.SemaphoreType.DMA
    act_shape = jax.ShapeDtypeStruct((mbs, mtok, dim), BF16)
    hid_shape = jax.ShapeDtypeStruct((chunks, CHUNK, ffn), BF16)
    return pl.pallas_call(
        functools.partial(step_kernel, n_stage),
        out_shape=(
            jax.ShapeDtypeStruct((chunks, CHUNK, ffn), F32), hid_shape, hid_shape,
            act_shape, act_shape, act_shape, act_shape,
            jax.ShapeDtypeStruct((rows, mbs * mtok), BF16),
            jax.ShapeDtypeStruct((rows, dim), F32),
            jax.ShapeDtypeStruct((8, 128), F32),
        ),
        in_specs=[vmem_spec] + [any_spec] * 4,
        out_specs=(any_spec,) * 9 + (vmem_spec,),
        scratch_shapes=[
            pltpu.VMEM((rows, dim), BF16), pltpu.VMEM((dim, ffn), BF16), pltpu.VMEM((ffn, dim), BF16),
            act, act, act, act, act, act,
            pltpu.VMEM((2, CHUNK, ffn), F32), pltpu.VMEM((2, CHUNK, ffn), BF16),
            pltpu.VMEM((rounds, n_stage, 8, tokens), F32), pltpu.VMEM((1, tokens), F32),
            dma((3,)), dma((mbs,)), dma((chunks,)), dma((chunks,)), dma((chunks,)), dma((chunks,)),
            dma((chunks,)), dma((chunks,)), dma((3, chunks)), dma((chunks,)),
            dma((rounds, n_stage)), dma((rounds, n_stage)), dma((mbs,)), dma((mbs,)), dma((mbs,)),
            dma((chunks,)), dma((chunks,)), dma((3, chunks)), dma((chunks,)),
            dma((2,)), dma((2,)), dma((2,)), dma((2,)), dma((2,)), dma((chunks,)),
        ],
        compiler_params=pltpu.CompilerParams(collective_id=0, has_side_effects=True, vmem_limit_bytes=VMEM_LIMIT),
        name="pipeline_step",
    )(labels, part, emb, w1, w2)


PACK = 256
TAIL_STEPS = 12


def tail_kernel(
    rows, tok_ref, x_hbm, g_hbm, gx_hbm, dpre_ref, hid_ref, ge_ref,
    g1_ref, g2_ref, out_ref,
    x_buf, g_buf, x_t, packed, packed_id, count_ref, sem,
):
    i = pl.program_id(0)
    mbs, mtok = tok_ref.shape
    total, dim = g_buf.shape
    n_pack = total // PACK
    e_rows = out_ref.shape[0]
    x_load = pltpu.make_async_copy(x_hbm, x_buf, sem.at[0])
    g_load = pltpu.make_async_copy(g_hbm, g_buf, sem.at[1])
    gx_load = pltpu.make_async_copy(gx_hbm, x_buf, sem.at[2])

    @pl.when(i == 0)
    def _():
        x_load.start()
        g_load.start()
        x_load.wait()
        x_t[...] = x_buf[...].T
        gx_load.start()
        g_load.wait()

        s = lax.axis_index("stage")
        loc = tok_ref[...] - s * rows
        here = (loc >= 0) & (loc < rows)
        flag = here.astype(F32)
        upper = (lax.broadcasted_iota(jnp.int32, (mtok, mtok), 0) <= lax.broadcasted_iota(jnp.int32, (mtok, mtok), 1))
        within = dot_nn(flag.astype(BF16), upper.astype(BF16))
        total_row = jnp.sum(flag, axis=1, keepdims=True)
        lower = (lax.broadcasted_iota(jnp.int32, (mbs, mbs), 1) < lax.broadcasted_iota(jnp.int32, (mbs, mbs), 0))
        before = jnp.sum(jnp.where(lower, jnp.transpose(jnp.broadcast_to(total_row, (mbs, mbs))), 0.0), axis=1, keepdims=True)
        slot_of = jnp.where(here, within - 1.0 + before, -1.0).astype(jnp.int32)
        count = jnp.sum(flag).astype(jnp.int32)
        count_ref[0] = count
        gx_load.wait()

        for b in range(n_pack):
            @pl.when(b * PACK < jnp.maximum(count, 1))
            def _(b=b):
                slot = lax.broadcasted_iota(jnp.int32, (PACK, mtok), 0) + b * PACK
                acc = jnp.zeros((PACK, dim), F32)
                ids = jnp.zeros((PACK, 1), F32)
                for mb in range(mbs):
                    pick = slot == slot_of[mb:mb + 1, :]
                    acc = acc + dot_nn(pick.astype(BF16), x_buf[pl.ds(mb * mtok, mtok), :])
                    ids = ids + jnp.sum(jnp.where(pick, loc[mb:mb + 1, :].astype(F32), 0.0), axis=1, keepdims=True)
                filled = lax.broadcasted_iota(jnp.int32, (PACK, 1), 0) + b * PACK < count
                packed[b] = acc.astype(BF16)
                packed_id[b] = jnp.broadcast_to(jnp.where(filled, ids.astype(jnp.int32), -1), (PACK, 128))

    g1_ref[0] = dot_nn(x_t[...], dpre_ref[...])
    g2_ref[0] = dot_tn(hid_ref[...], g_buf[...])
    lane = lax.broadcasted_iota(jnp.int32, (PACK, e_rows), 1) + i * e_rows

    def match_of(b):
        return (lane == packed_id[b][:, 0:1]).astype(BF16)

    out_ref[...] = ge_ref[...] + dot_tn(match_of(0), packed[0])

    def add_pack(b, _):
        out_ref[...] = out_ref[...] + dot_tn(match_of(b), packed[b])
        return 0

    lax.fori_loop(1, (count_ref[0] + PACK - 1) // PACK, add_pack, 0)


def tail(tok, x, g, gx, dpre, hid, ge):
    rows, dim = ge.shape
    total, ffn = dpre.shape
    mbs, mtok = tok.shape
    width = ffn // TAIL_STEPS
    e_rows = -(-rows // (TAIL_STEPS * 16)) * 16
    any_spec = pl.BlockSpec(memory_space=pl.ANY)
    dma = pltpu.SemaphoreType.DMA
    return pl.pallas_call(
        functools.partial(tail_kernel, rows),
        grid=(TAIL_STEPS,),
        out_shape=(
            jax.ShapeDtypeStruct((1, dim, ffn), F32),
            jax.ShapeDtypeStruct((1, ffn, dim), F32),
            jax.ShapeDtypeStruct((rows, dim), F32),
        ),
        in_specs=[
            pl.BlockSpec((mbs, mtok), lambda i: (0, 0)), any_spec, any_spec, any_spec,
            pl.BlockSpec((total, width), lambda i: (0, i)),
            pl.BlockSpec((total, width), lambda i: (0, i)),
            pl.BlockSpec((e_rows, dim), lambda i: (i, 0)),
        ],
        out_specs=(
            pl.BlockSpec((1, dim, width), lambda i: (0, 0, i)),
            pl.BlockSpec((1, width, dim), lambda i: (0, i, 0)),
            pl.BlockSpec((e_rows, dim), lambda i: (i, 0)),
        ),
        scratch_shapes=[
            pltpu.VMEM((total, dim), BF16), pltpu.VMEM((total, dim), BF16), pltpu.VMEM((dim, total), BF16),
            pltpu.VMEM((total // PACK, PACK, dim), BF16), pltpu.VMEM((total // PACK, PACK, 128), jnp.int32),
            pltpu.SMEM((1,), jnp.int32), dma((3,)),
        ],
        compiler_params=pltpu.CompilerParams(vmem_limit_bytes=60_000_000),
        name="tail",
    )(tok, x, g, gx, dpre, hid, ge)


def solution(mesh):
    n_stage = mesh.shape["stage"]

    def stage_body(token_ids, label_ids, emb_rows, w_in, w_out):
        stage_idx = lax.axis_index("stage")
        mbs, mtok = token_ids.shape
        rows, dim = emb_rows.shape
        ffn = w_in.shape[2]
        tokens = mbs * mtok
        local_tok = token_ids - stage_idx * rows
        tok_here = (local_tok >= 0) & (local_tok < rows)
        looked_up = jnp.take(emb_rows, jnp.clip(local_tok, 0, rows - 1), axis=0)
        part = jnp.where(tok_here[..., None], looked_up, 0)

        _, hid, dpre, x_in, _, g_all, gx, _, ge, loss = pipeline_step(n_stage, label_ids, part, emb_rows, w_in[0], w_out[0])
        flat = lambda a: a.reshape(tokens, a.shape[-1])
        grad_in, grad_out, grad_emb = tail(token_ids, flat(x_in), flat(g_all), flat(gx), flat(dpre), flat(hid), ge)
        mean_loss = (loss[0, 0] / tokens).reshape(1)
        return mean_loss, grad_in, grad_out, grad_emb

    return jax.shard_map(
        stage_body,
        mesh=mesh,
        in_specs=(P("dp", None), P("dp", None), P("stage", None), P("stage", None, None), P("stage", None, None)),
        out_specs=(P("dp"), P(("dp", "stage"), None, None), P(("dp", "stage"), None, None), P(("dp", "stage"), None)),
        check_vma=False,
    )
```

time: 1840 us -> 297 us (0.16)
  waiting for transfers between devices: 740 us -> 0 us
  matrix products: 492 us -> 0 us
  Pallas kernels: 0 us -> 271 us
  blocking collectives: 202 us -> 0 us
  other arithmetic: 145 us -> 3.45 us
  starting transfers between devices: 113 us -> 0 us
  local copies, waits for them, and re-layouts: 120 us -> 14.7 us
    dot_general x72 -> x0, matrix products: 492 us -> none  [the longest x8 151 us: head_step(): jnp.einsum('tv,td->vd', grad_logits, normed_mb, preferred_element_type=jn...]
    psum x11 -> x0, waiting for transfers between devices: 490 us -> none  [the longest x8 281 us: head_step(): lax.psum(jnp.einsum('tv,vd->td', grad_logits, emb_rows, preferred_element...]
    pallas_call x0 -> x2, Pallas kernels: none -> 271 us  [the longest x1 226 us: pipeline_step(): pl.pallas_call(functools.partial(step_kernel, n_stage), out_shape=(jax.Sh...]
    ppermute x30 -> x0, waiting for transfers between devices: 249 us -> none  [the longest x15 154 us: bwd_tick(): lax.ppermute(grad_in, 'stage', bwd_pairs)]
    ppermute x30 -> x0, starting transfers between devices: 112 us -> none  [the longest x15 62.1 us: bwd_tick(): lax.ppermute(grad_in, 'stage', bwd_pairs)]
    pmax x8 -> x0, blocking collectives: 102 us -> none  [head_step(): row_max = lax.pmax(jnp.max(logits, axis=1), 'stage')]
    psum x8 -> x0, blocking collectives: 100 us -> none  [head_step(): lax.psum(jnp.stack([jnp.sum(exp_logits, axis=1), jnp.sum(jnp.where(is_lab...]
    dynamic_update_slice x45 -> x0, other arithmetic: 45.6 us -> none  [put_slot(): lax.dynamic_update_index_in_dim(store_arr, jnp.where(active, new_value, o...]
  transfers between devices with their start and end apart: 41 -> 0, of which waited for: 41 -> 0; matrix products, arithmetic and copies ran while one was open for 10% -> 0% of each run, Pallas kernels for 0% -> 0%
where the time goes in v2:
time: 297 us; the launch traced here: 292 us
  Pallas kernels  271 us (91%)
  local copies, waits for them, and re-layouts  14.7 us (5%)
  other arithmetic  3.45 us (1%)
    pallas_call x1, Pallas kernels, pipeline_step(): pl.pallas_call(functools.partial(step_kernel, n_stage), out_shape=(jax.Sh...  226 us
    pallas_call x1, Pallas kernels, tail(): pl.pallas_call(functools.partial(tail_kernel, rows), grid=(TAIL_STEPS,),...  45.4 us
    gather x1, local copies, waits for them, and re-layouts, stage_body(): looked_up = jnp.take(emb_rows, jnp.clip(local_tok, 0, rows - 1), axis=0)  13.4 us

profile of v2, /device:TPU:122, one launch (start us, length us, event | category | flops | bytes accessed | tf_op | source)
XLA Modules:
  0.0 292.0 jit_solution(10514236636601128878)
XLA Ops:
  0.6 0.7 compare_and_fusion.1
  1.3 0.7 fusion
  2.1 13.4 %gather_fusion = bf16[2048,768]{1,0:T(8,128)(2,1)S(1)} fusion(bf16[6288,768]{1,0:T(8,128)(2,1)} %emb_hbm.1, s32[2048]{0:T(1024)S(1)} %broadcast_clamp_fusion), kind=kCustom, calls=%fused_computation | custom fusion | bytes 6299648 | tf_op jit(solution)/shard_map/jit(_take)/gather | solution.py:814
  15.5 2.0 select_select_fusion.part_hbm
  17.6 226.0 %pipeline_step.1 = (f32[16,128,3072]{2,1,0:T(8,128)}, bf16[16,128,3072]{2,1,0:T(8,128)(2,1)}, bf16[16,128,3072]{2,1,0:T(8,128)(2,1)}, bf16[8,256,768]{2,1,0:T(8,...) custom-call(s32[8,256]{1,0:T(8,128)} %lab_ref.1, ...), custom_call_target="tpu_custom_call" | custom-call | tf_op jit(solution)/shard_map/pipeline_step/pallas_call | solution.py:668
  243.6 1.2 slice.3
  245.4 45.4 %tail.1 = (f32[1,768,3072]{2,1,0:T(8,128)}, f32[1,3072,768]{2,1,0:T(8,128)}, f32[6288,768]{1,0:T(8,128)}) custom-call(s32[8,256]{1,0:T(8,128)} %tok_ref.1, bf16[2048,768]{1,0:T(8,128)(2,1)} %bitcast.17, bf16[2048,768]{1,0:T(8,128)(2,1)} %bitcast.18, bf16[2048,768]{1,0:T(8,128)(2,1)} %bitcast.19, bf16[2048,3072]{1,0:T(8,128)(2,1)} %bitcast.13, ...), custom_call_target="tpu_custom_call" | custom-call | tf_op jit(solution)/shard_map/tail/pallas_call | solution.py:774
  (2 shorter events, 0.0 us)

commit v3 on v2

--- a/solution.py
+++ b/solution.py
@@ -140,6 +140,121 @@
         part = dot_tn(d_log, emb[at, :])
         total = part if total is None else total + part
     return total
+
+
+LOOK = 160
+
+
+def look_at(w):
+    return pl.ds(w * LOOK if isinstance(w, int) else pl.multiple_of(w * LOOK, 16), LOOK)
+
+
+def ranks(flag, upper, lower):
+    within = dot_nn(flag.astype(BF16), upper)
+    total = jnp.sum(flag, axis=1, keepdims=True)
+    rows = flag.shape[0]
+    before = jnp.sum(jnp.where(lower, jnp.transpose(jnp.broadcast_to(total, (rows, rows))), 0.0), axis=1, keepdims=True)
+    return within - flag + before, jnp.sum(flag).astype(jnp.int32)
+
+
+def triangles(mbs, mtok):
+    upper = (lax.broadcasted_iota(jnp.int32, (mtok, mtok), 0)
+             <= lax.broadcasted_iota(jnp.int32, (mtok, mtok), 1)).astype(BF16)
+    lower = lax.broadcasted_iota(jnp.int32, (mbs, mbs), 1) < lax.broadcasted_iota(jnp.int32, (mbs, mbs), 0)
+    return upper, lower
+
+
+def lookup_kernel(tok_ref, emb_hbm, part_hbm, emb, part, rank_ref, picks, found, emb_sem, part_sem):
+    mbs, mtok = tok_ref.shape
+    rows, dim = emb.shape
+    tile = vocab_tile(rows)
+    n_tiles = rows // tile
+    loads = [pltpu.make_async_copy(emb_hbm.at[pl.ds(i * tile, tile)], emb.at[pl.ds(i * tile, tile)], emb_sem.at[i])
+             for i in range(n_tiles)]
+    for ld in loads:
+        ld.start()
+
+    loc = tok_ref[...] - lax.axis_index("stage") * rows
+    upper, lower = triangles(mbs, mtok)
+    counts = []
+    for i in range(n_tiles):
+        inside = (loc >= i * tile) & (loc < (i + 1) * tile)
+        rank, number = ranks(inside.astype(F32), upper, lower)
+        rank_ref[i] = jnp.where(inside, rank, -1.0).astype(jnp.int32)
+        counts.append(number)
+
+    def window(i, k, w):
+        slot = lax.broadcasted_iota(jnp.int32, (LOOK, mtok), 0) + k * LOOK
+        ids = jnp.zeros((LOOK, 1), F32)
+        for mb in range(mbs):
+            pick = slot == rank_ref[i, mb:mb + 1, :]
+            picks[mb, look_at(w), :] = pick.astype(BF16)
+            ids = ids + jnp.sum(jnp.where(pick, loc[mb:mb + 1, :].astype(F32), 0.0), axis=1, keepdims=True)
+        filled = lax.broadcasted_iota(jnp.int32, (LOOK, 1), 0) + k * LOOK < counts[i]
+        return jnp.where(filled, ids.astype(jnp.int32), -1)
+
+    def find(i, w, ids):
+        lane = lax.broadcasted_iota(jnp.int32, (LOOK, tile), 1) + i * tile
+        rows_found = dot_nn((lane == ids).astype(BF16), emb[pl.ds(i * tile, tile), :])
+        found[look_at(w), :] = rows_found.astype(BF16)
+
+    first_ids = [window(i, 0, i) for i in range(n_tiles)]
+    for i in range(n_tiles):
+        loads[i].wait()
+        find(i, i, first_ids[i])
+
+    n_windows = jnp.int32(n_tiles)
+    for i in range(n_tiles):
+        def extra(k, w, i=i):
+            find(i, w, window(i, k, w))
+            return w + 1
+        n_windows = lax.fori_loop(1, (counts[i] + LOOK - 1) // LOOK, extra, n_windows)
+
+    def save(mb):
+        return pltpu.make_async_copy(part.at[mb], part_hbm.at[mb], part_sem.at[mb])
+
+    base = n_tiles * LOOK
+    for mb in range(mbs):
+        part[mb] = dot_tn(picks[mb, 0:base, :], found[0:base, :]).astype(BF16)
+
+        @pl.when(n_windows == n_tiles)
+        def _(mb=mb):
+            save(mb).start()
+
+    @pl.when(n_windows > n_tiles)
+    def _():
+        for mb in range(mbs):
+            def add(w, _, mb=mb):
+                at = look_at(w)
+                part[mb] = part[mb] + dot_tn(picks[mb, at, :], found[at, :]).astype(BF16)
+                return 0
+            lax.fori_loop(n_tiles, n_windows, add, 0)
+            save(mb).start()
+
+    for mb in range(mbs):
+        save(mb).wait()
+
+
+def lookup(tok, emb):
+    mbs, mtok = tok.shape
+    rows, dim = emb.shape
+    n_tiles = rows // vocab_tile(rows)
+    slots = (n_tiles + mbs * mtok // LOOK) * LOOK
+    any_spec = pl.BlockSpec(memory_space=pl.ANY)
+    dma = pltpu.SemaphoreType.DMA
+    return pl.pallas_call(
+        lookup_kernel,
+        out_shape=jax.ShapeDtypeStruct((mbs, mtok, dim), BF16),
+        in_specs=[pl.BlockSpec(memory_space=pltpu.VMEM), any_spec],
+        out_specs=any_spec,
+        scratch_shapes=[
+            pltpu.VMEM((rows, dim), BF16), pltpu.VMEM((mbs, mtok, dim), BF16), pltpu.VMEM((n_tiles, mbs, mtok), jnp.int32),
+            pltpu.VMEM((mbs, slots, mtok), BF16), pltpu.VMEM((slots, dim), BF16),
+            dma((n_tiles,)), dma((mbs,)),
+        ],
+        compiler_params=pltpu.CompilerParams(vmem_limit_bytes=VMEM_LIMIT),
+        name="lookup",
+    )(tok, emb)
 
 
 E_ROWS = 512
@@ -692,132 +807,214 @@
     )(labels, part, emb, w1, w2)
 
 
-PACK = 256
-TAIL_STEPS = 12
+WINDOW = 256
+W_COLS = 1024
+E_SLOTS = 4
 
 
 def tail_kernel(
-    rows, tok_ref, x_hbm, g_hbm, gx_hbm, dpre_ref, hid_ref, ge_ref,
-    g1_ref, g2_ref, out_ref,
-    x_buf, g_buf, x_t, packed, packed_id, count_ref, sem,
+    rows, tok_ref, loss_ref, x_hbm, g_hbm, gx_hbm, dpre_hbm, hid_hbm, ge_hbm,
+    loss_out, g1_out, g2_out, out_hbm,
+    x_buf, g_buf, gx_buf, dp_buf, hid_buf, g1_stg, g2_stg, e_buf, packed, packed_id, bounds,
+    act_sem, dp_sem, hid_sem, g1_sem, g2_sem, e_in_sem, e_out_sem,
 ):
-    i = pl.program_id(0)
     mbs, mtok = tok_ref.shape
     total, dim = g_buf.shape
-    n_pack = total // PACK
-    e_rows = out_ref.shape[0]
-    x_load = pltpu.make_async_copy(x_hbm, x_buf, sem.at[0])
-    g_load = pltpu.make_async_copy(g_hbm, g_buf, sem.at[1])
-    gx_load = pltpu.make_async_copy(gx_hbm, x_buf, sem.at[2])
-
-    @pl.when(i == 0)
-    def _():
-        x_load.start()
-        g_load.start()
-        x_load.wait()
-        x_t[...] = x_buf[...].T
-        gx_load.start()
-        g_load.wait()
-
-        s = lax.axis_index("stage")
-        loc = tok_ref[...] - s * rows
-        here = (loc >= 0) & (loc < rows)
-        flag = here.astype(F32)
-        upper = (lax.broadcasted_iota(jnp.int32, (mtok, mtok), 0) <= lax.broadcasted_iota(jnp.int32, (mtok, mtok), 1))
-        within = dot_nn(flag.astype(BF16), upper.astype(BF16))
-        total_row = jnp.sum(flag, axis=1, keepdims=True)
-        lower = (lax.broadcasted_iota(jnp.int32, (mbs, mbs), 1) < lax.broadcasted_iota(jnp.int32, (mbs, mbs), 0))
-        before = jnp.sum(jnp.where(lower, jnp.transpose(jnp.broadcast_to(total_row, (mbs, mbs))), 0.0), axis=1, keepdims=True)
-        slot_of = jnp.where(here, within - 1.0 + before, -1.0).astype(jnp.int32)
-        count = jnp.sum(flag).astype(jnp.int32)
-        count_ref[0] = count
-        gx_load.wait()
-
-        for b in range(n_pack):
-            @pl.when(b * PACK < jnp.maximum(count, 1))
-            def _(b=b):
-                slot = lax.broadcasted_iota(jnp.int32, (PACK, mtok), 0) + b * PACK
-                acc = jnp.zeros((PACK, dim), F32)
-                ids = jnp.zeros((PACK, 1), F32)
-                for mb in range(mbs):
-                    pick = slot == slot_of[mb:mb + 1, :]
-                    acc = acc + dot_nn(pick.astype(BF16), x_buf[pl.ds(mb * mtok, mtok), :])
-                    ids = ids + jnp.sum(jnp.where(pick, loc[mb:mb + 1, :].astype(F32), 0.0), axis=1, keepdims=True)
-                filled = lax.broadcasted_iota(jnp.int32, (PACK, 1), 0) + b * PACK < count
-                packed[b] = acc.astype(BF16)
-                packed_id[b] = jnp.broadcast_to(jnp.where(filled, ids.astype(jnp.int32), -1), (PACK, 128))
-
-    g1_ref[0] = dot_nn(x_t[...], dpre_ref[...])
-    g2_ref[0] = dot_tn(hid_ref[...], g_buf[...])
-    lane = lax.broadcasted_iota(jnp.int32, (PACK, e_rows), 1) + i * e_rows
-
-    def match_of(b):
-        return (lane == packed_id[b][:, 0:1]).astype(BF16)
-
-    out_ref[...] = ge_ref[...] + dot_tn(match_of(0), packed[0])
-
-    def add_pack(b, _):
-        out_ref[...] = out_ref[...] + dot_tn(match_of(b), packed[b])
-        return 0
-
-    lax.fori_loop(1, (count_ref[0] + PACK - 1) // PACK, add_pack, 0)
-
-
-def tail(tok, x, g, gx, dpre, hid, ge):
+    ffn = dpre_hbm.shape[1]
+    n_blocks = ffn // W_COLS
+    e_rows = e_buf.shape[1]
+    n_e = rows // e_rows
+    per_block = n_e // n_blocks
+
+    def cols(j):
+        return pl.ds(pl.multiple_of(j * W_COLS, W_COLS), W_COLS)
+
+    def e_at(i):
+        return pl.ds(pl.multiple_of(i * e_rows, 8), e_rows)
+
+    def dp_load(j):
+        slot = lax.rem(j, 2)
+        return pltpu.make_async_copy(dpre_hbm.at[:, cols(j)], dp_buf.at[slot], dp_sem.at[slot])
+
+    def hid_load(j):
+        slot = lax.rem(j, 2)
+        return pltpu.make_async_copy(hid_hbm.at[:, cols(j)], hid_buf.at[slot], hid_sem.at[slot])
+
+    def e_load(i):
+        slot = lax.rem(i, E_SLOTS)
+        return pltpu.make_async_copy(ge_hbm.at[e_at(i)], e_buf.at[slot], e_in_sem.at[slot])
+
+    def e_save(i):
+        slot = lax.rem(i, E_SLOTS)
+        return pltpu.make_async_copy(e_buf.at[slot], out_hbm.at[e_at(i)], e_out_sem.at[slot])
+
+    def g1_save(j):
+        return pltpu.make_async_copy(g1_stg, g1_out.at[0, :, cols(j)], g1_sem.at[0])
+
+    def g2_save(j):
+        return pltpu.make_async_copy(g2_stg, g2_out.at[0, cols(j)], g2_sem.at[0])
+
+    x_load = pltpu.make_async_copy(x_hbm, x_buf, act_sem.at[0])
+    g_load = pltpu.make_async_copy(g_hbm, g_buf, act_sem.at[1])
+    gx_load = pltpu.make_async_copy(gx_hbm, gx_buf, act_sem.at[2])
+    gx_load.start()
+    loss_out[0] = loss_ref[0, 0] * (1.0 / total)
+
+    s = lax.axis_index("stage")
+    loc = tok_ref[...] - s * rows
+    upper, lower = triangles(mbs, mtok)
+    slot_of = jnp.full((mbs, mtok), -1.0, F32)
+    count = jnp.int32(0)
+    bounds[0] = count
+    for i in range(n_e):
+        inside = (loc >= i * e_rows) & (loc < (i + 1) * e_rows)
+        rank, number = ranks(inside.astype(F32), upper, lower)
+        slot_of = jnp.where(inside, rank + count.astype(F32), slot_of)
+        count = count + number
+        bounds[i + 1] = count
+    slot_of = slot_of.astype(jnp.int32)
+    n_packs = jnp.maximum((count + WINDOW - 1) // WINDOW, 1)
+
+    def pack(b):
+        slot = lax.broadcasted_iota(jnp.int32, (WINDOW, mtok), 0) + b * WINDOW
+        ids = jnp.zeros((WINDOW, 1), F32)
+        picks = []
+        for mb in range(mbs):
+            pick = slot == slot_of[mb:mb + 1, :]
+            picks.append(pick.astype(BF16))
+            ids = ids + jnp.sum(jnp.where(pick, loc[mb:mb + 1, :].astype(F32), 0.0), axis=1, keepdims=True)
+        at = pl.ds(pl.multiple_of(b * WINDOW, WINDOW), WINDOW)
+        packed[at, :] = dot_nn(jnp.concatenate(picks, axis=1), gx_buf[...]).astype(BF16)
+        filled = lax.broadcasted_iota(jnp.int32, (WINDOW, 1), 0) + b * WINDOW < count
+        packed_id[at, :] = jnp.broadcast_to(jnp.where(filled, ids.astype(jnp.int32), -1), (WINDOW, 128))
+
+    def loop(lo, hi, fn):
+        def body(i, _):
+            fn(i)
+            return 0
+        lax.fori_loop(lo, hi, body, 0)
+
+    def e_tile(i):
+        slot = lax.rem(i, E_SLOTS)
+        first = jnp.minimum((bounds[i] // 16) * 16, (n_packs - 1) * WINDOW)
+        lane = lax.broadcasted_iota(jnp.int32, (WINDOW, e_rows), 1) + i * e_rows
+
+        def window(k):
+            start = pl.multiple_of(jnp.minimum(first + k * WINDOW, (n_packs - 1) * WINDOW), 16)
+            at = pl.ds(start, WINDOW)
+            fresh = lax.broadcasted_iota(jnp.int32, (WINDOW, 1), 0) + start >= first + k * WINDOW
+            ids = jnp.where(fresh, packed_id[at, :][:, 0:1], -1)
+            return dot_tn((lane == ids).astype(BF16), packed[at, :])
+
+        e_load(i).wait()
+        e_buf[slot] = e_buf[slot] + window(0)
+
+        def more(k):
+            e_buf[slot] = e_buf[slot] + window(k)
+
+        loop(1, (bounds[i + 1] - first + WINDOW - 1) // WINDOW, more)
+        e_save(i).start()
+
+    def block(j):
+        slot = lax.rem(j, 2)
+
+        @pl.when(j == 0)
+        def _():
+            x_load.wait()
+
+        @pl.when(j > 0)
+        def _():
+            g1_save(j - 1).wait()
+        dp_load(j).wait()
+
+        @pl.when(j == 0)
+        def _():
+            for cp in (e_load(0), e_load(1), g_load, hid_load(0)):
+                cp.start()
+        g1_stg[...] = dot_tn(x_buf[...], dp_buf[slot])
+        g1_save(j).start()
+
+        @pl.when(j + 1 < n_blocks)
+        def _():
+            dp_load(j + 1).start()
+
+        def tile(i):
+            @pl.when(i + 2 < n_e)
+            def _():
+                @pl.when(i + 2 >= E_SLOTS)
+                def _():
+                    e_save(i + 2 - E_SLOTS).wait()
+                e_load(i + 2).start()
+            e_tile(i)
+
+        loop(j * per_block, (j + 1) * per_block, tile)
+
+        @pl.when(j == 0)
+        def _():
+            g_load.wait()
+
+        @pl.when(j > 0)
+        def _():
+            g2_save(j - 1).wait()
+        hid_load(j).wait()
+
+        @pl.when(j + 1 < n_blocks)
+        def _():
+            hid_load(j + 1).start()
+        g2_stg[...] = dot_tn(hid_buf[slot], g_buf[...])
+        g2_save(j).start()
+
+    x_load.start()
+    dp_load(0).start()
+    gx_load.wait()
+    loop(0, n_packs, pack)
+    loop(0, n_blocks, block)
+    g1_save(n_blocks - 1).wait()
+    g2_save(n_blocks - 1).wait()
+    for i in range(max(n_e - E_SLOTS, 0), n_e):
+        e_save(i).wait()
+
+
+def tail(tok, loss, x, g, gx, dpre, hid, ge):
     rows, dim = ge.shape
     total, ffn = dpre.shape
-    mbs, mtok = tok.shape
-    width = ffn // TAIL_STEPS
-    e_rows = -(-rows // (TAIL_STEPS * 16)) * 16
+    n_blocks = ffn // W_COLS
+    e_rows = rows // (2 * n_blocks)
+    n_e = rows // e_rows
     any_spec = pl.BlockSpec(memory_space=pl.ANY)
+    vmem_spec = pl.BlockSpec(memory_space=pltpu.VMEM)
     dma = pltpu.SemaphoreType.DMA
+    act = pltpu.VMEM((total, dim), BF16)
     return pl.pallas_call(
         functools.partial(tail_kernel, rows),
-        grid=(TAIL_STEPS,),
         out_shape=(
+            jax.ShapeDtypeStruct((1,), F32),
             jax.ShapeDtypeStruct((1, dim, ffn), F32),
             jax.ShapeDtypeStruct((1, ffn, dim), F32),
             jax.ShapeDtypeStruct((rows, dim), F32),
         ),
-        in_specs=[
-            pl.BlockSpec((mbs, mtok), lambda i: (0, 0)), any_spec, any_spec, any_spec,
-            pl.BlockSpec((total, width), lambda i: (0, i)),
-            pl.BlockSpec((total, width), lambda i: (0, i)),
-            pl.BlockSpec((e_rows, dim), lambda i: (i, 0)),
+        in_specs=[vmem_spec, vmem_spec] + [any_spec] * 6,
+        out_specs=(pl.BlockSpec(memory_space=pltpu.SMEM), any_spec, any_spec, any_spec),
+        scratch_shapes=[
+            act, act, act, pltpu.VMEM((2, total, W_COLS), BF16), pltpu.VMEM((2, total, W_COLS), BF16),
+            pltpu.VMEM((dim, W_COLS), F32), pltpu.VMEM((W_COLS, dim), F32), pltpu.VMEM((E_SLOTS, e_rows, dim), F32),
+            pltpu.VMEM((total, dim), BF16), pltpu.VMEM((total, 128), jnp.int32), pltpu.SMEM((n_e + 1,), jnp.int32),
+            dma((3,)), dma((2,)), dma((2,)), dma((1,)), dma((1,)), dma((E_SLOTS,)), dma((E_SLOTS,)),
         ],
-        out_specs=(
-            pl.BlockSpec((1, dim, width), lambda i: (0, 0, i)),
-            pl.BlockSpec((1, width, dim), lambda i: (0, i, 0)),
-            pl.BlockSpec((e_rows, dim), lambda i: (i, 0)),
-        ),
-        scratch_shapes=[
-            pltpu.VMEM((total, dim), BF16), pltpu.VMEM((total, dim), BF16), pltpu.VMEM((dim, total), BF16),
-            pltpu.VMEM((total // PACK, PACK, dim), BF16), pltpu.VMEM((total // PACK, PACK, 128), jnp.int32),
-            pltpu.SMEM((1,), jnp.int32), dma((3,)),
-        ],
-        compiler_params=pltpu.CompilerParams(vmem_limit_bytes=60_000_000),
+        compiler_params=pltpu.CompilerParams(vmem_limit_bytes=VMEM_LIMIT),
         name="tail",
-    )(tok, x, g, gx, dpre, hid, ge)
+    )(tok, loss, x, g, gx, dpre, hid, ge)
 
 
 def solution(mesh):
     n_stage = mesh.shape["stage"]
 
     def stage_body(token_ids, label_ids, emb_rows, w_in, w_out):
-        stage_idx = lax.axis_index("stage")
-        mbs, mtok = token_ids.shape
-        rows, dim = emb_rows.shape
-        ffn = w_in.shape[2]
-        tokens = mbs * mtok
-        local_tok = token_ids - stage_idx * rows
-        tok_here = (local_tok >= 0) & (local_tok < rows)
-        looked_up = jnp.take(emb_rows, jnp.clip(local_tok, 0, rows - 1), axis=0)
-        part = jnp.where(tok_here[..., None], looked_up, 0)
-
+        tokens = token_ids.shape[0] * token_ids.shape[1]
+        part = lookup(token_ids, emb_rows)
         _, hid, dpre, x_in, _, g_all, gx, _, ge, loss = pipeline_step(n_stage, label_ids, part, emb_rows, w_in[0], w_out[0])
         flat = lambda a: a.reshape(tokens, a.shape[-1])
-        grad_in, grad_out, grad_emb = tail(token_ids, flat(x_in), flat(g_all), flat(gx), flat(dpre), flat(hid), ge)
-        mean_loss = (loss[0, 0] / tokens).reshape(1)
+        mean_loss, grad_in, grad_out, grad_emb = tail(token_ids, loss, flat(x_in), flat(g_all), flat(gx), flat(dpre), flat(hid), ge)
         return mean_loss, grad_in, grad_out, grad_emb
 
     return jax.shard_map(

time: 297 us -> 274 us (0.923)
  local copies, waits for them, and re-layouts: 14.7 us -> 0 us
  other arithmetic: 3.45 us -> 0 us
  Pallas kernels: 271 us -> 268 us
    gather x1 -> x0, local copies, waits for them, and re-layouts: 13.4 us -> none  [stage_body(): looked_up = jnp.take(emb_rows, jnp.clip(local_tok, 0, rows - 1), axis=0)]
    pallas_call x1 -> x2, Pallas kernels: 45.4 us -> 42.2 us  [the longest x1 34 us: tail(): pl.pallas_call(functools.partial(tail_kernel, rows), out_shape=(jax.Shape...]
where the time goes in v3:
time: 274 us; the launch traced here: 269 us
  Pallas kernels  268 us (98%)
    pallas_call x1, Pallas kernels, pipeline_step(): pl.pallas_call(functools.partial(step_kernel, n_stage), out_shape=(jax.Sh...  226 us
    pallas_call x1, Pallas kernels, tail(): pl.pallas_call(functools.partial(tail_kernel, rows), out_shape=(jax.Shape...  34 us
    pallas_call x1, Pallas kernels, lookup(): pl.pallas_call(lookup_kernel, out_shape=jax.ShapeDtypeStruct((mbs, mtok,...  8.17 us

profile of v3, /device:TPU:122, one launch (start us, length us, event | category | flops | bytes accessed | tf_op | source)
XLA Modules:
  0.0 269.0 jit_solution(3141034881149808459)
XLA Ops:
  0.6 8.2 %lookup.1.part_hbm = bf16[8,256,768]{2,1,0:T(8,128)(2,1)} custom-call(s32[8,256]{1,0:T(8,128)} %tok_ref.3, bf16[6288,768]{1,0:T(8,128)(2,1)} %emb_hbm.3), custom_call_target="tpu_custom_call" | custom-call | tf_op jit(solution)/shard_map/lookup/pallas_call | solution.py:245
  8.8 226.0 %pipeline_step.1 = (f32[16,128,3072]{2,1,0:T(8,128)}, bf16[16,128,3072]{2,1,0:T(8,128)(2,1)}, bf16[16,128,3072]{2,1,0:T(8,128)(2,1)}, bf16[8,256,768]{2,1,0:T(8,...) custom-call(s32[8,256]{1,0:T(8,128)} %lab_ref.1, ...), custom_call_target="tpu_custom_call" | custom-call | tf_op jit(solution)/shard_map/pipeline_step/pallas_call | solution.py:783
  234.8 34.0 %tail.1 = (f32[1]{0:T(128)}, f32[1,768,3072]{2,1,0:T(8,128)}, f32[1,3072,768]{2,1,0:T(8,128)}, f32[6288,768]{1,0:T(8,128)}) custom-call(s32[8,256]{1,0:T(8,128)} %tok_ref.3, f32[8,128]{1,0:T(8,128)} %get-tuple-element.11.loss_ref, bf16[2048,768]{1,0:T(8,128)(2,1)} %bitcast.11, bf16[2048,768]{1,0:T(8,128)(2,1)} %bitcast.12, bf16[2048,768]{1,0:T(8,128)(2,1)} %bitcast.13, ...), custom_call_target="tpu_custom_call" | custom-call | tf_op jit(solution)/shard_map/tail/pallas_call | solution.py:988

commit v4 on v3

--- a/solution.py
+++ b/solution.py
@@ -80,22 +80,42 @@
     return x.astype(F32) + dot_nn(hid_slot[...], w2[...])
 
 
-def backward_chunk(grad, wt, slope_slot, dpre_slot):
+def forward_pair(x, w1, w2, slope_slots, hid_slots):
+    ffn = w1.shape[1]
+    width = ffn // 4
+    for part in range(4):
+        cols = pl.ds(part * width, width)
+        hid, slope = gelu_and_slope(dot_nn(x, w1[:, cols]))
+        for slot in range(2):
+            slope_slots[slot, :, cols] = slope[slot * CHUNK:(slot + 1) * CHUNK]
+            hid_slots[slot, :, cols] = hid[slot * CHUNK:(slot + 1) * CHUNK].astype(BF16)
+    return x.astype(F32) + dot_nn(hid_slots[...].reshape(2 * CHUNK, ffn), w2[...])
+
+
+def backward_chunk(grad, w2_t, w1_t, slope_slot, dpre_slot):
     ffn = slope_slot.shape[1]
     dim = grad.shape[1]
     for part in range(ffn // dim):
         cols = pl.ds(part * dim, dim)
-        d_hid = dot_nn(grad, wt[pl.ds(ffn + part * dim, dim), :])
-        dpre_slot[:, cols] = (d_hid * slope_slot[:, cols]).astype(BF16)
-    return grad.astype(F32) + dot_nn(dpre_slot[...], wt[pl.ds(0, ffn), :])
-
-
-def transpose_weights(w1, w2, wt):
+        dpre_slot[:, cols] = (dot_nn(grad, w2_t[:, cols]) * slope_slot[:, cols]).astype(BF16)
+    return grad.astype(F32) + dot_nn(dpre_slot[...], w1_t[...])
+
+
+def swap_transposed(w1, w2):
     dim, ffn = w1.shape
-    for part in range(ffn // dim):
-        at = pl.ds(part * dim, dim)
-        wt[at, :] = w1[:, at].T
-        wt[pl.ds(ffn + part * dim, dim), :] = w2[at, :].T
+    side = 256
+
+    def strip(part, _):
+        at = pl.ds(pl.multiple_of(part * side, side), side)
+        for i in range(dim // side):
+            rows = pl.ds(i * side, side)
+            from_w1 = w1[rows, at].T
+            from_w2 = w2[at, rows].T
+            w2[at, rows] = from_w1
+            w1[rows, at] = from_w2
+        return 0
+
+    lax.fori_loop(0, ffn // side, strip, 0)
 
 
 def head_logits(n_t, emb, logits, lab_row, tokens):
@@ -258,7 +278,7 @@
 
 
 E_ROWS = 512
-LOOKUP_LEAD = 1
+LOOKUP_LEAD = 8
 LOOKUP_PARENT = {2: (3, 0), 1: (0, 0), 4: (5, 0), 6: (7, 0), 5: (3, 1), 7: (0, 1), 3: (0, 2)}
 GRAD_PARENT = {0: (1, 0), 2: (3, 0), 4: (5, 0), 1: (6, 0), 6: (7, 0), 3: (5, 1), 5: (7, 1)}
 
@@ -288,10 +308,8 @@
 
     loads = [pltpu.make_async_copy(src, dst, load_sem.at[i])
              for i, (src, dst) in enumerate([(w1_hbm, w1), (w2_hbm, w2), (emb_hbm, emb)])]
-    for mb in range(mbs):
-        pltpu.make_async_copy(part_hbm.at[mb], comb.at[mb], part_sem.at[mb]).start()
-    for ld in loads:
-        ld.start()
+    part_load = pltpu.make_async_copy(part_hbm, comb, part_sem.at[0])
+    part_load.start()
     group_barrier(s, n_stage)
 
     def pos(c):
@@ -317,12 +335,12 @@
 
     def lk_copy(c, child):
         parent, slot = LOOKUP_PARENT[child]
-        return remote(at_chunk(comb, c), at_chunk(bufs[slot], c), lk_send.at[c], lk_sems[slot].at[c], parent)
+        return remote(at_chunk(comb, c), at_chunk(bufs[slot], c), lk_send.at[0], lk_sems[slot].at[c], parent)
 
     def lk_total(c, slots):
         total = comb[pos(c)].astype(F32)
         for slot in range(slots):
-            remote(at_chunk(comb, c), at_chunk(bufs[slot], c), lk_send.at[c], lk_sems[slot].at[c], 0).wait_recv()
+            remote(at_chunk(comb, c), at_chunk(bufs[slot], c), lk_send.at[0], lk_sems[slot].at[c], 0).wait_recv()
             total = total + bufs[slot][pos(c)].astype(F32)
         return total.astype(BF16)
 
@@ -330,27 +348,38 @@
         comb[pos(c)] = lk_total(c, slots)
         lk_copy(c, node).start()
 
-    loop(0, mbs, lambda mb: pltpu.make_async_copy(part_hbm.at[mb], comb.at[mb], part_sem.at[mb]).wait())
+    part_load.wait()
     each_role((1, 2, 4, 6), lambda node: loop(0, n_chunks, lambda c: lk_copy(c, node).start()))
+    for ld in loads:
+        ld.start()
     each_role((5, 7), lambda node: loop(0, n_chunks, lambda c: lk_forward(c, node, 1)))
+    each_role((3,), lambda node: loop(0, LOOKUP_LEAD, lambda c: lk_forward(c, node, 2)))
     loads[0].wait()
     loads[1].wait()
 
     n_routes = {last: (5, 1, 6), 5: (4,), 1: (3, 0), 3: (2,)}
 
     def x_copy(c, dst_stage):
-        return remote(at_chunk(x_out, c), at_chunk(x_in, c), x_send.at[c], x_recv.at[c], dst_stage)
+        return remote(at_chunk(x_out, c), at_chunk(x_in, c), x_send.at[0], x_recv.at[c], dst_stage)
 
     def n_copy(c, lane, dst_stage):
-        return remote(at_chunk(n_all, c), at_chunk(n_all, c), n_send.at[lane, c], n_recv.at[c], dst_stage)
+        return remote(at_chunk(n_all, c), at_chunk(n_all, c), n_send.at[lane], n_recv.at[c], dst_stage)
 
     def fwd_copies(c):
         slot = lax.rem(c, 2)
         return (pltpu.make_async_copy(slope_stg.at[slot], slope_out.at[c], slope_sem.at[slot]),
                 pltpu.make_async_copy(act_stg.at[slot], hid_out.at[c], act_sem.at[slot]))
 
+    def slope_copy(c):
+        slot = lax.rem(c, 2)
+        return pltpu.make_async_copy(slope_out.at[c], slope_stg.at[slot], slope_sem.at[slot])
+
     def fwd_chunk(c):
         idx = pos(c)
+
+        @pl.when((s == 3) & (c + LOOKUP_LEAD < n_chunks))
+        def _():
+            lk_forward(c + LOOKUP_LEAD, 3, 2)
 
         @pl.when(s == 0)
         def _():
@@ -379,6 +408,22 @@
         def _():
             out_f = out.astype(F32)
             n_all[idx] = (out_f * norm_scale(out_f)).astype(BF16)
+            for lane, dst in enumerate(n_routes[last]):
+                n_copy(c, lane, dst).start()
+
+    def last_fwd_pair(mb):
+        first = mb * n_half
+        for c in (first, first + 1):
+            x_copy(c, 0).wait_recv()
+            for cp in fwd_copies(c - 2):
+                cp.wait()
+        out = forward_pair(x_in[mb], w1, w2, slope_stg, act_stg).astype(BF16)
+        x_out[mb] = out
+        out_f = out.astype(F32)
+        n_all[mb] = (out_f * norm_scale(out_f)).astype(BF16)
+        for c in (first, first + 1):
+            for cp in fwd_copies(c):
+                cp.start()
             for lane, dst in enumerate(n_routes[last]):
                 n_copy(c, lane, dst).start()
 
@@ -405,12 +450,12 @@
 
     def g_copy(mb, child):
         parent, slot = GRAD_PARENT[child]
-        return remote(comb.at[mb], bufs[slot].at[mb], g_send.at[mb], (g_a, g_b)[slot].at[mb], parent)
+        return remote(comb.at[mb], bufs[slot].at[mb], g_send.at[0], (g_a, g_b)[slot].at[mb], parent)
 
     def g_total(mb, slots):
         total = comb[mb].astype(F32)
         for slot in range(slots):
-            remote(comb.at[mb], bufs[slot].at[mb], g_send.at[mb], (g_a, g_b)[slot].at[mb], 0).wait_recv()
+            remote(comb.at[mb], bufs[slot].at[mb], g_send.at[0], (g_a, g_b)[slot].at[mb], 0).wait_recv()
             total = total + bufs[slot][mb].astype(F32)
         return total
 
@@ -441,7 +486,7 @@
 
     def st_copy(r, off):
         dst = lax.rem(s + off, n_stage)
-        return remote(stats.at[r, s], stats.at[r, s], st_send.at[r, off], st_recv.at[r, off], dst)
+        return remote(stats.at[r, s], stats.at[r, s], st_send.at[0], st_recv.at[r], dst)
 
     saves = [pltpu.make_async_copy(x_in, xin_out, out_sem.at[0]), pltpu.make_async_copy(n_all, n_out, out_sem.at[1])]
 
@@ -464,13 +509,11 @@
                 for cp in saves:
                     cp.wait()
 
-                @pl.when(s < last)
-                def _():
-                    loop(0, n_chunks, lambda c: x_copy(c, 0).wait_send())
                 for src, dsts in n_routes.items():
                     @pl.when(s == src)
                     def _(dsts=dsts):
-                        loop(0, n_chunks, lambda c: [n_copy(c, lane, dst).wait_send() for lane, dst in enumerate(dsts)])
+                        for lane, dst in enumerate(dsts):
+                            remote(n_all, n_all, n_send.at[lane], n_recv.at[0], dst).wait_send()
             stats[r, s] = jnp.concatenate([top, tot, lab, jnp.zeros((5, tokens), F32)], axis=0)
             for off in range(1, n_stage):
                 st_copy(r, off).start()
@@ -486,9 +529,16 @@
             @pl.when(r + 1 < rounds)
             def _():
                 n_early(r + 1)
-            for off in range(1, n_stage):
-                src = lax.rem(s + n_stage - off, n_stage)
-                remote(stats.at[r, s], stats.at[r, src], st_send.at[r, off], st_recv.at[r, off], src).wait_recv()
+
+            @pl.when((r == rounds - 2) & (s < last))
+            def _():
+                remote(x_out, x_in, x_send.at[0], x_recv.at[0], 0).wait_send()
+
+            @pl.when(r == jnp.where(s == last, rounds - 1, rounds - 2))
+            def _():
+                swap_transposed(w1, w2)
+            others = stats.at[r, pl.ds(0, last)]
+            remote(others, others, st_send.at[0], st_recv.at[r], lax.rem(s + 1, n_stage)).wait_recv()
             blocks = [stats[r, i] for i in range(n_stage)]
             top = blocks[0][0:1]
             for blk in blocks[1:]:
@@ -524,19 +574,17 @@
         first_a = HEAD_MBS + 1 + last
 
         def step(k):
-            @pl.when((s == 3) & (k == 0))
-            def _():
-                loop(0, LOOKUP_LEAD * n_half, lambda c: lk_forward(c, 3, 2))
-
-            @pl.when((s == 3) & (k + LOOKUP_LEAD < mbs))
-            def _():
-                chunks_of(k + LOOKUP_LEAD, lambda c: lk_forward(c, 3, 2))
-
             f_mb = k - s
 
-            @pl.when((f_mb >= 0) & (f_mb < mbs))
+            paired = (s == last) & (f_mb >= 2 * HEAD_MBS)
+
+            @pl.when((f_mb >= 0) & (f_mb < mbs) & jnp.logical_not(paired))
             def _():
                 chunks_of(f_mb, fwd_chunk)
+
+            @pl.when((f_mb < mbs) & paired)
+            def _():
+                last_fwd_pair(f_mb)
 
             @pl.when(k == first_a)
             def _():
@@ -544,7 +592,7 @@
 
                 @pl.when(s > 0)
                 def _():
-                    loop(0, n_chunks, lambda c: lk_copy(c, 1).wait_send())
+                    remote(comb, buf_a, lk_send.at[0], lk_a.at[0], 0).wait_send()
 
             rel = k - first_a
             r = rel // HEAD_MBS
@@ -563,9 +611,9 @@
             def _():
                 g_low(r - 1)
 
-                @pl.when(r >= 2)
+                @pl.when(r == 2)
                 def _():
-                    loop((r - 2) * HEAD_MBS, (r - 1) * HEAD_MBS, g_final)
+                    loop(0, HEAD_MBS, g_final)
 
             @pl.when(jnp.logical_not(even) & (rel >= 0))
             def _():
@@ -579,6 +627,9 @@
         for c in (n_chunks - 2, n_chunks - 1):
             for cp in fwd_copies(c):
                 cp.wait()
+        slope_copy(0).start()
+        slope_copy(1).start()
+        g_low(rounds - 1)
         for seq in (rounds * n_tiles - 2, rounds * n_tiles - 1):
             d_copy(seq).wait()
 
@@ -589,25 +640,21 @@
     )
     loss_out[...] = jnp.broadcast_to(jnp.sum(loss_acc[...], axis=1, keepdims=True), loss_out.shape)
 
-    g_in, g_buf, gx, wt = x_in, x_out, n_all, emb
+    g_in, g_buf, gx = x_in, x_out, n_all
 
     def b_copy(c, dst):
-        return remote(at_chunk(g_buf, c), at_chunk(g_in, c), b_send.at[c], b_recv.at[c], dst)
+        return remote(at_chunk(g_buf, c), at_chunk(g_in, c), b_send.at[0], b_recv.at[c], dst)
 
     def gx_copy(c, lane, dst):
-        return remote(at_chunk(gx, c), at_chunk(gx, c), gx_send.at[lane, c], gx_recv.at[c], dst)
-
-    def slope_copy(c):
-        slot = lax.rem(c, 2)
-        return pltpu.make_async_copy(slope_out.at[c], slope_stg.at[slot], slope_sem.at[slot])
+        return remote(at_chunk(gx, c), at_chunk(gx, c), gx_send.at[lane], gx_recv.at[c], dst)
 
     def dpre_copy(c):
         slot = lax.rem(c, 2)
         return pltpu.make_async_copy(act_stg.at[slot], dpre_out.at[c], act_sem.at[slot])
 
     gx_split = n_chunks // 2
-    gx_routes = {0: ((3, 0, n_chunks), (last, 0, n_chunks), (1, 0, n_chunks)), 3: ((2, 0, n_chunks), (5, 0, gx_split)),
-                 last: ((6, 0, n_chunks), (5, gx_split, n_chunks)), 5: ((4, 0, n_chunks),)}
+    gx_routes = {0: ((5, n_chunks - 1, n_chunks), (3, 0, n_chunks), (last, 0, n_chunks), (1, 0, n_chunks)), 3: ((2, 0, n_chunks), (5, 0, gx_split)),
+                 last: ((6, 0, n_chunks), (5, gx_split, n_chunks - 1)), 5: ((4, 0, n_chunks),)}
 
     def gx_send_all(c, node):
         for lane, (dst, lo, hi) in enumerate(gx_routes[node]):
@@ -616,6 +663,9 @@
                 gx_copy(c, lane, dst).start()
 
 
+    def gx_save(c):
+        return pltpu.make_async_copy(at_chunk(gx, c), at_chunk(gx_out, c), gx_sem.at[0])
+
     def bwd_chunk(c):
         slot = lax.rem(c, 2)
         idx = pos(c)
@@ -632,7 +682,7 @@
         def _():
             dpre_copy(c - 2).wait()
         slope_copy(c).wait()
-        dx = backward_chunk(g_in[idx], wt, slope_stg.at[slot], act_stg.at[slot]).astype(BF16)
+        dx = backward_chunk(g_in[idx], w1, w2, slope_stg.at[slot], act_stg.at[slot]).astype(BF16)
 
         @pl.when(s > 0)
         def _():
@@ -643,6 +693,7 @@
         def _():
             gx[idx] = dx
             gx_send_all(c, 0)
+            gx_save(c).start()
         dpre_copy(c).start()
 
         @pl.when(c + 2 < n_chunks)
@@ -675,6 +726,10 @@
                     d_load(full, rest).start()
             d_load(i).wait()
 
+            @pl.when(i == 0)
+            def _():
+                n_load.wait()
+
             @pl.when(i >= 2)
             def _():
                 e_save(i - 2).wait()
@@ -683,33 +738,31 @@
 
         n_load = pltpu.make_async_copy(n_out, n_rows, out_sem.at[1])
         n_load.start()
-        slope_copy(0).start()
-        slope_copy(1).start()
         d_load(0).start()
-        g_low(rounds - 1)
-        transpose_weights(w1, w2, wt)
-        n_load.wait()
-        early = jnp.minimum((last - s) * 2, full)
+        early = jnp.where(s == last - 1, 0, jnp.minimum((last - s) * 2, full))
         loop(0, early, e_tile)
 
-        def gx_save(c):
-            return pltpu.make_async_copy(at_chunk(gx, c), at_chunk(gx_out, c), gx_sem.at[c])
+        def g_save(mb, count):
+            at = pl.ds(mb, count)
+            return pltpu.make_async_copy(g_in.at[at], g_out.at[at], out_sem.at[0])
 
         def gx_forward(c):
-            @pl.when(s > 0)
-            def _():
-                gx_copy(c, 0, 0).wait_recv()
+            gx_copy(c, 0, 0).wait_recv()
             each_role((3, last, 5), lambda node: gx_send_all(c, node))
             gx_save(c).start()
 
         def step(k):
-            @pl.when(k >= mbs - 2 * HEAD_MBS)
+            @pl.when(k >= HEAD_MBS)
             def _():
                 @pl.when(k < mbs)
                 def _():
                     g_final(k)
             b_mb = k - (last - s)
 
+            @pl.when(b_mb == mbs - 1)
+            def _():
+                g_save(0, mbs - 1).start()
+
             @pl.when((b_mb >= 0) & (b_mb < mbs))
             def _():
                 chunks_of(b_mb, bwd_chunk)
@@ -725,10 +778,8 @@
                 chunks_of(x_mb, gx_forward)
 
         loop(0, mbs + last, step)
-        g_save = pltpu.make_async_copy(g_in, g_out, out_sem.at[0])
-        g_save.start()
+        g_save(mbs - 1, 1).start()
         loop(early, full, e_tile)
-        loop(jnp.where(s == 3, gx_split, 0), n_chunks, gx_forward)
         if rest:
             d_load(full, rest).wait()
             e_save(full - 2).wait()
@@ -736,35 +787,39 @@
             e_stg[slot, pl.ds(0, rest)] = dot_nn(d_in[slot, pl.ds(0, rest)], n_rows[...].reshape(mbs * mtok, dim))
             e_save(full, rest).start()
 
-        g_save.wait()
+        loop(jnp.where(s == 0, n_chunks, jnp.where(s == 3, gx_split, 0)), n_chunks, gx_forward)
+
+        for c in (n_chunks - 2, n_chunks - 1):
+            dpre_copy(c).wait()
+        pltpu.make_async_copy(g_in, g_out, out_sem.at[0]).wait()
         if rest:
             e_save(full - 1).wait()
             e_save(full, rest).wait()
         else:
             e_save(full - 2).wait()
             e_save(full - 1).wait()
-        for c in (n_chunks - 2, n_chunks - 1):
-            dpre_copy(c).wait()
-        loop(0, n_chunks, lambda c: gx_save(c).wait())
+        pltpu.make_async_copy(gx, gx_out, gx_sem.at[0]).wait()
+        sent = stats.at[:, pl.ds(0, last)]
+        remote(sent, sent, st_send.at[0], st_recv.at[0], lax.rem(s + 1, n_stage)).wait_send()
+
+        @pl.when(s < last)
+        def _():
+            remote(comb, buf_a, g_send.at[0], g_a.at[0], last).wait_send()
+
+        @pl.when(s > 0)
+        def _():
+            remote(g_buf, g_in, b_send.at[0], b_recv.at[0], 0).wait_send()
+        for src, routes in gx_routes.items():
+            @pl.when(s == src)
+            def _(routes=routes):
+                for lane, (dst, lo, hi) in enumerate(routes):
+                    part = gx if hi - lo == n_chunks else gx.at[pl.ds(0, hi - lo), pl.ds(0, CHUNK)]
+                    remote(part, part, gx_send.at[lane], gx_recv.at[0], dst).wait_send()
 
     pl.run_scoped(
         backward,
         pltpu.VMEM((mbs, mtok, dim), BF16), pltpu.VMEM((2, E_ROWS, mbs * mtok), BF16), pltpu.VMEM((2, E_ROWS, dim), F32),
     )
-
-    @pl.when(s < last)
-    def _():
-        loop(0, mbs, lambda mb: g_copy(mb, 1).wait_send())
-
-    @pl.when(s > 0)
-    def _():
-        loop(0, n_chunks, lambda c: b_copy(c, 0).wait_send())
-    for src, routes in gx_routes.items():
-        @pl.when(s == src)
-        def _(routes=routes):
-            for lane, (dst, lo, hi) in enumerate(routes):
-                loop(lo, hi, lambda c: gx_copy(c, lane, dst).wait_send())
-    loop(0, rounds, lambda r: [st_copy(r, off).wait_send() for off in range(1, n_stage)])
 
 
 def pipeline_step(n_stage, labels, part, emb, w1, w2):
@@ -796,11 +851,10 @@
             act, act, act, act, act, act,
             pltpu.VMEM((2, CHUNK, ffn), F32), pltpu.VMEM((2, CHUNK, ffn), BF16),
             pltpu.VMEM((rounds, n_stage, 8, tokens), F32), pltpu.VMEM((1, tokens), F32),
-            dma((3,)), dma((mbs,)), dma((chunks,)), dma((chunks,)), dma((chunks,)), dma((chunks,)),
-            dma((chunks,)), dma((chunks,)), dma((3, chunks)), dma((chunks,)),
-            dma((rounds, n_stage)), dma((rounds, n_stage)), dma((mbs,)), dma((mbs,)), dma((mbs,)),
-            dma((chunks,)), dma((chunks,)), dma((3, chunks)), dma((chunks,)),
-            dma((2,)), dma((2,)), dma((2,)), dma((2,)), dma((2,)), dma((chunks,)),
+            dma((3,)), dma((1,)), dma((1,)), dma((chunks,)), dma((chunks,)), dma((chunks,)),
+            dma((1,)), dma((chunks,)), dma((3,)), dma((chunks,)), dma((1,)), dma((rounds,)),
+            dma((1,)), dma((mbs,)), dma((mbs,)), dma((1,)), dma((chunks,)), dma((4,)), dma((chunks,)),
+            dma((2,)), dma((2,)), dma((2,)), dma((2,)), dma((2,)), dma((1,)),
         ],
         compiler_params=pltpu.CompilerParams(collective_id=0, has_side_effects=True, vmem_limit_bytes=VMEM_LIMIT),
         name="pipeline_step",

time: 274 us -> 262 us (0.956); the launches traced: 269 us -> 261 us
  Pallas kernels: 268 us -> 260 us
    pallas_call x1, Pallas kernels: 226 us -> 218 us  [pipeline_step(): pl.pallas_call(functools.partial(step_kernel, n_stage), out_shape=(jax.Sh...]
where the time goes in v4:
time: 262 us; the launch traced here: 261 us
  Pallas kernels  260 us (99%)
    pallas_call x1, Pallas kernels, pipeline_step(): pl.pallas_call(functools.partial(step_kernel, n_stage), out_shape=(jax.Sh...  218 us
    pallas_call x1, Pallas kernels, tail(): pl.pallas_call(functools.partial(tail_kernel, rows), out_shape=(jax.Shape...  34 us
    pallas_call x1, Pallas kernels, lookup(): pl.pallas_call(lookup_kernel, out_shape=jax.ShapeDtypeStruct((mbs, mtok,...  8.17 us

profile of v4, /device:TPU:122, one launch (start us, length us, event | category | flops | bytes accessed | tf_op | source)
XLA Modules:
  0.0 261.1 jit_solution(17738788774826335706)
XLA Ops:
  0.6 8.2 %lookup.1.part_hbm = bf16[8,256,768]{2,1,0:T(8,128)(2,1)} custom-call(s32[8,256]{1,0:T(8,128)} %tok_ref.3, bf16[6288,768]{1,0:T(8,128)(2,1)} %emb_hbm.3), custom_call_target="tpu_custom_call" | custom-call | tf_op jit(solution)/shard_map/lookup/pallas_call | solution.py:265
  8.8 218.1 %pipeline_step.1 = (f32[16,128,3072]{2,1,0:T(8,128)}, bf16[16,128,3072]{2,1,0:T(8,128)(2,1)}, bf16[16,128,3072]{2,1,0:T(8,128)(2,1)}, bf16[8,256,768]{2,1,0:T(8,...) custom-call(s32[8,256]{1,0:T(8,128)} %lab_ref.1, ...), custom_call_target="tpu_custom_call" | custom-call | tf_op jit(solution)/shard_map/pipeline_step/pallas_call | solution.py:838
  226.9 34.0 %tail.1 = (f32[1]{0:T(128)}, f32[1,768,3072]{2,1,0:T(8,128)}, f32[1,3072,768]{2,1,0:T(8,128)}, f32[6288,768]{1,0:T(8,128)}) custom-call(s32[8,256]{1,0:T(8,128)} %tok_ref.3, f32[8,128]{1,0:T(8,128)} %get-tuple-element.11.loss_ref, bf16[2048,768]{1,0:T(8,128)(2,1)} %bitcast.11, bf16[2048,768]{1,0:T(8,128)(2,1)} %bitcast.12, bf16[2048,768]{1,0:T(8,128)(2,1)} %bitcast.13, ...), custom_call_target="tpu_custom_call" | custom-call | tf_op jit(solution)/shard_map/tail/pallas_call | solution.py:1042

commit v5 on v4

--- a/solution.py
+++ b/solution.py
@@ -162,11 +162,12 @@
     return total
 
 
-LOOK = 160
-
-
-def look_at(w):
-    return pl.ds(w * LOOK if isinstance(w, int) else pl.multiple_of(w * LOOK, 16), LOOK)
+LOOK = 192
+LOOK_BASE = 512
+
+
+def look_at(row):
+    return pl.ds(pl.multiple_of(row, 16), LOOK)
 
 
 def ranks(flag, upper, lower):
@@ -194,6 +195,8 @@
     for ld in loads:
         ld.start()
 
+    picks[:, pl.ds(0, LOOK_BASE + LOOK), :] = jnp.zeros((mbs, LOOK_BASE + LOOK, mtok), BF16)
+    found[pl.ds(0, LOOK_BASE + LOOK), :] = jnp.zeros((LOOK_BASE + LOOK, dim), BF16)
     loc = tok_ref[...] - lax.axis_index("stage") * rows
     upper, lower = triangles(mbs, mtok)
     counts = []
@@ -203,53 +206,59 @@
         rank_ref[i] = jnp.where(inside, rank, -1.0).astype(jnp.int32)
         counts.append(number)
 
-    def window(i, k, w):
+    def window(i, k, row):
         slot = lax.broadcasted_iota(jnp.int32, (LOOK, mtok), 0) + k * LOOK
         ids = jnp.zeros((LOOK, 1), F32)
         for mb in range(mbs):
             pick = slot == rank_ref[i, mb:mb + 1, :]
-            picks[mb, look_at(w), :] = pick.astype(BF16)
+            picks[mb, look_at(row), :] = pick.astype(BF16)
             ids = ids + jnp.sum(jnp.where(pick, loc[mb:mb + 1, :].astype(F32), 0.0), axis=1, keepdims=True)
         filled = lax.broadcasted_iota(jnp.int32, (LOOK, 1), 0) + k * LOOK < counts[i]
         return jnp.where(filled, ids.astype(jnp.int32), -1)
 
-    def find(i, w, ids):
+    def find(i, row, ids):
         lane = lax.broadcasted_iota(jnp.int32, (LOOK, tile), 1) + i * tile
         rows_found = dot_nn((lane == ids).astype(BF16), emb[pl.ds(i * tile, tile), :])
-        found[look_at(w), :] = rows_found.astype(BF16)
-
-    first_ids = [window(i, 0, i) for i in range(n_tiles)]
+        found[look_at(row), :] = rows_found.astype(BF16)
+
+    starts = [jnp.int32(0)]
+    for number in counts:
+        starts.append(starts[-1] + (jnp.minimum(number, LOOK) + 15) // 16 * 16)
+    first_ids = [window(i, 0, starts[i]) for i in range(n_tiles)]
     for i in range(n_tiles):
         loads[i].wait()
-        find(i, i, first_ids[i])
-
-    n_windows = jnp.int32(n_tiles)
+        find(i, starts[i], first_ids[i])
+
+    extra_end = jnp.int32(1)
     for i in range(n_tiles):
         def extra(k, w, i=i):
-            find(i, w, window(i, k, w))
+            row = LOOK_BASE + w * LOOK
+            find(i, row, window(i, k, row))
             return w + 1
-        n_windows = lax.fori_loop(1, (counts[i] + LOOK - 1) // LOOK, extra, n_windows)
+        extra_end = lax.fori_loop(1, (counts[i] + LOOK - 1) // LOOK, extra, extra_end)
+    crowded = (extra_end > 1) | (starts[n_tiles] > LOOK_BASE)
 
     def save(mb):
         return pltpu.make_async_copy(part.at[mb], part_hbm.at[mb], part_sem.at[mb])
 
-    base = n_tiles * LOOK
     for mb in range(mbs):
-        part[mb] = dot_tn(picks[mb, 0:base, :], found[0:base, :]).astype(BF16)
-
-        @pl.when(n_windows == n_tiles)
+        part[mb] = dot_tn(picks[mb, 0:LOOK_BASE, :], found[0:LOOK_BASE, :]).astype(BF16)
+
+        @pl.when(jnp.logical_not(crowded))
         def _(mb=mb):
             save(mb).start()
 
-    @pl.when(n_windows > n_tiles)
+    @pl.when(crowded)
     def _():
-        for mb in range(mbs):
-            def add(w, _, mb=mb):
-                at = look_at(w)
+        def add_mb(mb, _):
+            def add(w, _):
+                at = look_at(LOOK_BASE + w * LOOK)
                 part[mb] = part[mb] + dot_tn(picks[mb, at, :], found[at, :]).astype(BF16)
                 return 0
-            lax.fori_loop(n_tiles, n_windows, add, 0)
+            lax.fori_loop(0, extra_end, add, 0)
             save(mb).start()
+            return 0
+        lax.fori_loop(0, mbs, add_mb, 0)
 
     for mb in range(mbs):
         save(mb).wait()
@@ -259,7 +268,7 @@
     mbs, mtok = tok.shape
     rows, dim = emb.shape
     n_tiles = rows // vocab_tile(rows)
-    slots = (n_tiles + mbs * mtok // LOOK) * LOOK
+    slots = LOOK_BASE + (1 + mbs * mtok // LOOK) * LOOK
     any_spec = pl.BlockSpec(memory_space=pl.ANY)
     dma = pltpu.SemaphoreType.DMA
     return pl.pallas_call(
@@ -278,6 +287,8 @@
 
 
 E_ROWS = 512
+LATE_TILES = 3
+EARLY_TILES = (11, 9, 8, 6, 4, 3, 0, 0)
 LOOKUP_LEAD = 8
 LOOKUP_PARENT = {2: (3, 0), 1: (0, 0), 4: (5, 0), 6: (7, 0), 5: (3, 1), 7: (0, 1), 3: (0, 2)}
 GRAD_PARENT = {0: (1, 0), 2: (3, 0), 4: (5, 0), 1: (6, 0), 6: (7, 0), 3: (5, 1), 5: (7, 1)}
@@ -286,9 +297,9 @@
 def step_kernel(
     n_stage, lab_ref, part_hbm, emb_hbm, w1_hbm, w2_hbm,
     slope_out, hid_out, dpre_out, xin_out, n_out, g_out, gx_out, dt_out, ge_out, loss_out,
-    emb, w1, w2, x_in, x_out, n_all, comb, buf_a, buf_b, slope_stg, act_stg, stats, loss_acc,
+    emb, w1, w2, x_in, x_out, n_all, comb, buf_a, buf_b, slope_stg, act_stg, d_stg, stats, loss_acc,
     load_sem, part_sem, lk_send, lk_a, lk_b, lk_c, x_send, x_recv, n_send, n_recv, st_send, st_recv,
-    g_send, g_a, g_b, b_send, b_recv, gx_send, gx_recv, slope_sem, act_sem, d_sem, e_sem, out_sem, gx_sem,
+    g_send, g_a, g_b, b_send, b_recv, gx_send, gx_recv, slope_sem, act_sem, dt_sem, d_sem, e_sem, out_sem, gx_sem,
 ):
     s = lax.axis_index("stage")
     last = n_stage - 1
@@ -466,9 +477,8 @@
     def g_low(r):
         each_role((1, 3), lambda node: loop(r * HEAD_MBS, (r + 1) * HEAD_MBS, lambda mb: g_forward(mb, node, 1)))
 
-    def g_mid(r):
-        each_role((6,), lambda node: loop(r * HEAD_MBS, (r + 1) * HEAD_MBS, lambda mb: g_forward(mb, node, 1)))
-        each_role((5,), lambda node: loop(r * HEAD_MBS, (r + 1) * HEAD_MBS, lambda mb: g_forward(mb, node, 2)))
+    def g_mid(r, nodes=(5, 6)):
+        each_role(nodes, lambda node: loop(r * HEAD_MBS, (r + 1) * HEAD_MBS, lambda mb: g_forward(mb, node, {5: 2, 6: 1}[node])))
 
     def g_final(mb):
         @pl.when(s == last)
@@ -490,9 +500,16 @@
 
     saves = [pltpu.make_async_copy(x_in, xin_out, out_sem.at[0]), pltpu.make_async_copy(n_all, n_out, out_sem.at[1])]
 
-    def forward_and_head(logits, n_t, d_stg, gn_acc):
-        n_tiles = rows // tile
-
+    n_tiles = rows // tile
+
+    def d_copy(seq):
+        slot = lax.rem(seq, 2)
+        r = seq // n_tiles
+        idx = lax.rem(seq, n_tiles)
+        dst = dt_out.at[pl.ds(pl.multiple_of(idx * tile, 16), tile), pl.ds(pl.multiple_of(r * tokens, tokens), tokens)]
+        return pltpu.make_async_copy(d_stg.at[slot], dst, dt_sem.at[slot])
+
+    def forward_and_head(logits, n_t, gn_acc):
         def head_a(r):
             n_late(r)
 
@@ -518,13 +535,6 @@
             for off in range(1, n_stage):
                 st_copy(r, off).start()
 
-        def d_copy(seq):
-            slot = lax.rem(seq, 2)
-            r = seq // n_tiles
-            idx = lax.rem(seq, n_tiles)
-            dst = dt_out.at[pl.ds(pl.multiple_of(idx * tile, 16), tile), pl.ds(pl.multiple_of(r * tokens, tokens), tokens)]
-            return pltpu.make_async_copy(d_stg.at[slot], dst, d_sem.at[slot])
-
         def head_b(r):
             @pl.when(r + 1 < rounds)
             def _():
@@ -533,6 +543,14 @@
             @pl.when((r == rounds - 2) & (s < last))
             def _():
                 remote(x_out, x_in, x_send.at[0], x_recv.at[0], 0).wait_send()
+
+            @pl.when(r == rounds - 1)
+            def _():
+                for c in (n_chunks - 2, n_chunks - 1):
+                    for cp in fwd_copies(c):
+                        cp.wait()
+                slope_copy(0).start()
+                slope_copy(1).start()
 
             @pl.when(r == jnp.where(s == last, rounds - 1, rounds - 2))
             def _():
@@ -624,21 +642,12 @@
                 g_mid(r - 1)
 
         loop(0, first_a + HEAD_MBS * rounds, step)
-        for c in (n_chunks - 2, n_chunks - 1):
-            for cp in fwd_copies(c):
-                cp.wait()
-        slope_copy(0).start()
-        slope_copy(1).start()
         g_low(rounds - 1)
-        for seq in (rounds * n_tiles - 2, rounds * n_tiles - 1):
-            d_copy(seq).wait()
 
     pl.run_scoped(
         forward_and_head,
-        pltpu.VMEM((rows, tokens), F32), pltpu.VMEM((dim, tokens), BF16),
-        pltpu.VMEM((2, tile, tokens), BF16), pltpu.VMEM((tokens, dim), F32),
+        pltpu.VMEM((rows, tokens), F32), pltpu.VMEM((dim, tokens), BF16), pltpu.VMEM((tokens, dim), F32),
     )
-    loss_out[...] = jnp.broadcast_to(jnp.sum(loss_acc[...], axis=1, keepdims=True), loss_out.shape)
 
     g_in, g_buf, gx = x_in, x_out, n_all
 
@@ -738,8 +747,18 @@
 
         n_load = pltpu.make_async_copy(n_out, n_rows, out_sem.at[1])
         n_load.start()
-        d_load(0).start()
-        early = jnp.where(s == last - 1, 0, jnp.minimum((last - s) * 2, full))
+
+        def table_start():
+            for seq in (rounds * n_tiles - 2, rounds * n_tiles - 1):
+                d_copy(seq).wait()
+            d_load(0).start()
+
+        @pl.when(s < last)
+        def _():
+            table_start()
+        early = jnp.int32(0)
+        for node, tiles in enumerate(EARLY_TILES):
+            early = early + jnp.where(s == node, min(tiles, full), 0)
         loop(0, early, e_tile)
 
         def g_save(mb, count):
@@ -769,7 +788,11 @@
 
             @pl.when(k == 2)
             def _():
-                g_mid(rounds - 1)
+                g_mid(rounds - 1, (5,))
+
+            @pl.when(k == 4)
+            def _():
+                g_mid(rounds - 1, (6,))
 
             x_mb = k - n_stage
 
@@ -779,19 +802,52 @@
 
         loop(0, mbs + last, step)
         g_save(mbs - 1, 1).start()
-        loop(early, full, e_tile)
-        if rest:
-            d_load(full, rest).wait()
-            e_save(full - 2).wait()
-            slot = full % 2
-            e_stg[slot, pl.ds(0, rest)] = dot_nn(d_in[slot, pl.ds(0, rest)], n_rows[...].reshape(mbs * mtok, dim))
-            e_save(full, rest).start()
-
-        loop(jnp.where(s == 0, n_chunks, jnp.where(s == 3, gx_split, 0)), n_chunks, gx_forward)
-
-        for c in (n_chunks - 2, n_chunks - 1):
-            dpre_copy(c).wait()
-        pltpu.make_async_copy(g_in, g_out, out_sem.at[0]).wait()
+
+        @pl.when(s == last)
+        def _():
+            table_start()
+        kept = jnp.where(s == last, LATE_TILES, 0)
+        before = full - early - kept
+        first_gx = jnp.where(s == 3, gx_split, 0)
+
+        def late(j):
+            c = first_gx + j - before
+
+            @pl.when((j >= before) & (s > 0))
+            def _():
+                gx_forward(c)
+            i = jnp.where(j < before, early + j, full - kept + c - gx_split)
+
+            @pl.when((j < before) | ((c >= gx_split) & (i < full)))
+            def _():
+                e_tile(i)
+            if rest:
+                @pl.when(c == gx_split + kept)
+                def _():
+                    d_load(full, rest).wait()
+                    e_save(full - 2).wait()
+                    slot = full % 2
+                    e_stg[slot, pl.ds(0, rest)] = dot_nn(d_in[slot, pl.ds(0, rest)], n_rows[...].reshape(mbs * mtok, dim))
+                    e_save(full, rest).start()
+
+            @pl.when(c == n_chunks - 3)
+            def _():
+                loss_out[...] = jnp.broadcast_to(jnp.sum(loss_acc[...], axis=1, keepdims=True), loss_out.shape)
+                for c in (n_chunks - 2, n_chunks - 1):
+                    dpre_copy(c).wait()
+                pltpu.make_async_copy(g_in, g_out, out_sem.at[0]).wait()
+                sent = stats.at[:, pl.ds(0, last)]
+                remote(sent, sent, st_send.at[0], st_recv.at[0], lax.rem(s + 1, n_stage)).wait_send()
+
+                @pl.when(s < last)
+                def _():
+                    remote(comb, buf_a, g_send.at[0], g_a.at[0], last).wait_send()
+
+                @pl.when(s > 0)
+                def _():
+                    remote(g_buf, g_in, b_send.at[0], b_recv.at[0], 0).wait_send()
+
+        loop(0, before + n_chunks - first_gx, late)
         if rest:
             e_save(full - 1).wait()
             e_save(full, rest).wait()
@@ -799,16 +855,6 @@
             e_save(full - 2).wait()
             e_save(full - 1).wait()
         pltpu.make_async_copy(gx, gx_out, gx_sem.at[0]).wait()
-        sent = stats.at[:, pl.ds(0, last)]
-        remote(sent, sent, st_send.at[0], st_recv.at[0], lax.rem(s + 1, n_stage)).wait_send()
-
-        @pl.when(s < last)
-        def _():
-            remote(comb, buf_a, g_send.at[0], g_a.at[0], last).wait_send()
-
-        @pl.when(s > 0)
-        def _():
-            remote(g_buf, g_in, b_send.at[0], b_recv.at[0], 0).wait_send()
         for src, routes in gx_routes.items():
             @pl.when(s == src)
             def _(routes=routes):
@@ -850,11 +896,11 @@
             pltpu.VMEM((rows, dim), BF16), pltpu.VMEM((dim, ffn), BF16), pltpu.VMEM((ffn, dim), BF16),
             act, act, act, act, act, act,
             pltpu.VMEM((2, CHUNK, ffn), F32), pltpu.VMEM((2, CHUNK, ffn), BF16),
-            pltpu.VMEM((rounds, n_stage, 8, tokens), F32), pltpu.VMEM((1, tokens), F32),
+            pltpu.VMEM((2, vocab_tile(rows), tokens), BF16), pltpu.VMEM((rounds, n_stage, 8, tokens), F32), pltpu.VMEM((1, tokens), F32),
             dma((3,)), dma((1,)), dma((1,)), dma((chunks,)), dma((chunks,)), dma((chunks,)),
             dma((1,)), dma((chunks,)), dma((3,)), dma((chunks,)), dma((1,)), dma((rounds,)),
             dma((1,)), dma((mbs,)), dma((mbs,)), dma((1,)), dma((chunks,)), dma((4,)), dma((chunks,)),
-            dma((2,)), dma((2,)), dma((2,)), dma((2,)), dma((2,)), dma((1,)),
+            dma((2,)), dma((2,)), dma((2,)), dma((2,)), dma((2,)), dma((2,)), dma((1,)),
         ],
         compiler_params=pltpu.CompilerParams(collective_id=0, has_side_effects=True, vmem_limit_bytes=VMEM_LIMIT),
         name="pipeline_step",

time: 262 us -> 259 us (0.989)
    pallas_call x1, Pallas kernels: 218 us -> 215 us  [pipeline_step(): pl.pallas_call(functools.partial(step_kernel, n_stage), out_shape=(jax.Sh...]
where the time goes in v5:
time: 259 us; the launch traced here: 258 us
  Pallas kernels  258 us (100%)
    pallas_call x1, Pallas kernels, pipeline_step(): pl.pallas_call(functools.partial(step_kernel, n_stage), out_shape=(jax.Sh...  215 us
    pallas_call x1, Pallas kernels, tail(): pl.pallas_call(functools.partial(tail_kernel, rows), out_shape=(jax.Shape...  34 us
    pallas_call x1, Pallas kernels, lookup(): pl.pallas_call(lookup_kernel, out_shape=jax.ShapeDtypeStruct((mbs, mtok,...  8.81 us

profile of v5, /device:TPU:122, one launch (start us, length us, event | category | flops | bytes accessed | tf_op | source)
XLA Modules:
  0.0 258.3 jit_solution(11842045885234610098)
XLA Ops:
  0.6 8.8 %lookup.1.part_hbm = bf16[8,256,768]{2,1,0:T(8,128)(2,1)} custom-call(s32[8,256]{1,0:T(8,128)} %tok_ref.3, bf16[6288,768]{1,0:T(8,128)(2,1)} %emb_hbm.3), custom_call_target="tpu_custom_call" | custom-call | tf_op jit(solution)/shard_map/lookup/pallas_call | solution.py:274
  9.5 214.7 %pipeline_step.1 = (f32[16,128,3072]{2,1,0:T(8,128)}, bf16[16,128,3072]{2,1,0:T(8,128)(2,1)}, bf16[16,128,3072]{2,1,0:T(8,128)(2,1)}, bf16[8,256,768]{2,1,0:T(8,...) custom-call(s32[8,256]{1,0:T(8,128)} %lab_ref.1, ...), custom_call_target="tpu_custom_call" | custom-call | tf_op jit(solution)/shard_map/pipeline_step/pallas_call | solution.py:884
  224.1 34.0 %tail.1 = (f32[1]{0:T(128)}, f32[1,768,3072]{2,1,0:T(8,128)}, f32[1,3072,768]{2,1,0:T(8,128)}, f32[6288,768]{1,0:T(8,128)}) custom-call(s32[8,256]{1,0:T(8,128)} %tok_ref.3, f32[8,128]{1,0:T(8,128)} %get-tuple-element.11.loss_ref, bf16[2048,768]{1,0:T(8,128)(2,1)} %bitcast.11, bf16[2048,768]{1,0:T(8,128)(2,1)} %bitcast.12, bf16[2048,768]{1,0:T(8,128)(2,1)} %bitcast.13, ...), custom_call_target="tpu_custom_call" | custom-call | tf_op jit(solution)/shard_map/tail/pallas_call | solution.py:1088

commit v6 on v5

--- a/solution.py
+++ b/solution.py
@@ -147,14 +147,14 @@
     return top, tot, lab
 
 
-def head_grad_tile(base, size_all, emb, logits, d_slot, lab_row, top, shift, tokens):
+def head_grad_tile(base, size_all, emb, logits, d_slot, lab_row, shift, tokens):
     scale = emb.shape[1] ** -0.5
     c2 = LOG2E * scale
     total = None
     for start, size in sub_blocks(size_all, 256):
         at = pl.ds(base + start, size)
         row_ids = lax.broadcasted_iota(jnp.int32, (size, tokens), 0) + (base + start)
-        prob = jnp.exp2((logits[at, :] - top) * c2 - shift)
+        prob = jnp.exp2(logits[at, :] * c2 - shift)
         d_log = (prob - jnp.where(row_ids == lab_row, scale, 0.0)).astype(BF16)
         d_slot[pl.ds(start, size), :] = d_log
         part = dot_tn(d_log, emb[at, :])
@@ -567,7 +567,7 @@
                 tot = tot + blk[1:2] * jnp.exp2((blk[0:1] - top) * c2)
                 lab = lab + blk[2:3]
             loss_acc[...] = loss_acc[...] + (jnp.log(tot) + (top - lab) * scale)
-            shift = jnp.log(tot) * LOG2E - math.log2(scale)
+            shift = top * c2 + (jnp.log(tot) * LOG2E - math.log2(scale))
             lab_row = lab_row_of(r)
 
             def tile_step(idx):
@@ -580,7 +580,7 @@
                 def _():
                     n_mid(r + 1)
                 base = pl.multiple_of(idx * tile, 16)
-                part = head_grad_tile(base, tile, emb, logits, d_stg.at[lax.rem(seq, 2)], lab_row, top, shift, tokens)
+                part = head_grad_tile(base, tile, emb, logits, d_stg.at[lax.rem(seq, 2)], lab_row, shift, tokens)
                 gn_acc[...] = gn_acc[...] + part
                 d_copy(seq).start()
 

time: 259 us -> 258 us (level)
  no operation moved by 1% of the time
where the time goes in v6:
time: 258 us; the launch traced here: 257 us
  Pallas kernels  257 us (100%)
    pallas_call x1, Pallas kernels, pipeline_step(): pl.pallas_call(functools.partial(step_kernel, n_stage), out_shape=(jax.Sh...  214 us
    pallas_call x1, Pallas kernels, tail(): pl.pallas_call(functools.partial(tail_kernel, rows), out_shape=(jax.Shape...  34 us
    pallas_call x1, Pallas kernels, lookup(): pl.pallas_call(lookup_kernel, out_shape=jax.ShapeDtypeStruct((mbs, mtok,...  8.81 us

profile of v6, /device:TPU:122, one launch (start us, length us, event | category | flops | bytes accessed | tf_op | source)
XLA Modules:
  0.0 257.4 jit_solution(4446391643067172110)
XLA Ops:
  0.6 8.8 %lookup.1.part_hbm = bf16[8,256,768]{2,1,0:T(8,128)(2,1)} custom-call(s32[8,256]{1,0:T(8,128)} %tok_ref.3, bf16[6288,768]{1,0:T(8,128)(2,1)} %emb_hbm.3), custom_call_target="tpu_custom_call" | custom-call | tf_op jit(solution)/shard_map/lookup/pallas_call | solution.py:274
  9.5 213.7 %pipeline_step.1 = (f32[16,128,3072]{2,1,0:T(8,128)}, bf16[16,128,3072]{2,1,0:T(8,128)(2,1)}, bf16[16,128,3072]{2,1,0:T(8,128)(2,1)}, bf16[8,256,768]{2,1,0:T(8,...) custom-call(s32[8,256]{1,0:T(8,128)} %lab_ref.1, ...), custom_call_target="tpu_custom_call" | custom-call | tf_op jit(solution)/shard_map/pipeline_step/pallas_call | solution.py:884
  223.2 34.0 %tail.1 = (f32[1]{0:T(128)}, f32[1,768,3072]{2,1,0:T(8,128)}, f32[1,3072,768]{2,1,0:T(8,128)}, f32[6288,768]{1,0:T(8,128)}) custom-call(s32[8,256]{1,0:T(8,128)} %tok_ref.3, f32[8,128]{1,0:T(8,128)} %get-tuple-element.11.loss_ref, bf16[2048,768]{1,0:T(8,128)(2,1)} %bitcast.11, bf16[2048,768]{1,0:T(8,128)(2,1)} %bitcast.12, bf16[2048,768]{1,0:T(8,128)(2,1)} %bitcast.13, ...), custom_call_target="tpu_custom_call" | custom-call | tf_op jit(solution)/shard_map/tail/pallas_call | solution.py:1088

commit v7 on v6

--- a/solution.py
+++ b/solution.py
@@ -1038,16 +1038,7 @@
         def _():
             dp_load(j + 1).start()
 
-        def tile(i):
-            @pl.when(i + 2 < n_e)
-            def _():
-                @pl.when(i + 2 >= E_SLOTS)
-                def _():
-                    e_save(i + 2 - E_SLOTS).wait()
-                e_load(i + 2).start()
-            e_tile(i)
-
-        loop(j * per_block, (j + 1) * per_block, tile)
+        loop(j * per_block, (j + 1) * per_block, e_tile)
 
         @pl.when(j == 0)
         def _():
@@ -1061,6 +1052,16 @@
         @pl.when(j + 1 < n_blocks)
         def _():
             hid_load(j + 1).start()
+
+        def ahead(i):
+            @pl.when(i >= E_SLOTS)
+            def _():
+                e_save(i - E_SLOTS).wait()
+            e_load(i).start()
+
+        @pl.when(j + 1 < n_blocks)
+        def _():
+            loop((j + 1) * per_block, (j + 2) * per_block, ahead)
         g2_stg[...] = dot_tn(hid_buf[slot], g_buf[...])
         g2_save(j).start()
 

time: 258 us -> 258 us (level)
  no operation moved by 1% of the time
where the time goes in v7:
time: 258 us
  Pallas kernels  257 us (100%)
    pallas_call x1, Pallas kernels, pipeline_step(): pl.pallas_call(functools.partial(step_kernel, n_stage), out_shape=(jax.Sh...  214 us
    pallas_call x1, Pallas kernels, tail(): pl.pallas_call(functools.partial(tail_kernel, rows), out_shape=(jax.Shape...  34.2 us
    pallas_call x1, Pallas kernels, lookup(): pl.pallas_call(lookup_kernel, out_shape=jax.ShapeDtypeStruct((mbs, mtok,...  8.81 us

profile of v7, /device:TPU:122, one launch (start us, length us, event | category | flops | bytes accessed | tf_op | source)
XLA Modules:
  0.0 257.6 jit_solution(11741199646318330182)
XLA Ops:
  0.6 8.8 %lookup.1.part_hbm = bf16[8,256,768]{2,1,0:T(8,128)(2,1)} custom-call(s32[8,256]{1,0:T(8,128)} %tok_ref.3, bf16[6288,768]{1,0:T(8,128)(2,1)} %emb_hbm.3), custom_call_target="tpu_custom_call" | custom-call | tf_op jit(solution)/shard_map/lookup/pallas_call | solution.py:274
  9.5 213.7 %pipeline_step.1 = (f32[16,128,3072]{2,1,0:T(8,128)}, bf16[16,128,3072]{2,1,0:T(8,128)(2,1)}, bf16[16,128,3072]{2,1,0:T(8,128)(2,1)}, bf16[8,256,768]{2,1,0:T(8,...) custom-call(s32[8,256]{1,0:T(8,128)} %lab_ref.1, ...), custom_call_target="tpu_custom_call" | custom-call | tf_op jit(solution)/shard_map/pipeline_step/pallas_call | solution.py:884
  223.2 34.2 %tail.1 = (f32[1]{0:T(128)}, f32[1,768,3072]{2,1,0:T(8,128)}, f32[1,3072,768]{2,1,0:T(8,128)}, f32[6288,768]{1,0:T(8,128)}) custom-call(s32[8,256]{1,0:T(8,128)} %tok_ref.3, f32[8,128]{1,0:T(8,128)} %get-tuple-element.11.loss_ref, bf16[2048,768]{1,0:T(8,128)(2,1)} %bitcast.11, bf16[2048,768]{1,0:T(8,128)(2,1)} %bitcast.12, bf16[2048,768]{1,0:T(8,128)(2,1)} %bitcast.13, ...), custom_call_target="tpu_custom_call" | custom-call | tf_op jit(solution)/shard_map/tail/pallas_call | solution.py:1089
